TPU v7x, 256 devices: a whole 4x4x8 slice. The times are simulated.
256 devices in a mesh: dp: 256 (over y, x, z, core).
Axes of the slice: x: 4, y: 4, z: 8, core: 2. Of those that a mesh axis runs over, the one named last changes fastest.
Arguments:
- features: bfloat16 [2048, 128, 1024], P('dp'), may hold values from -16 to 16
- ln_gain: float32 [1024], replicated, may hold values from 0.5 to 1.5
- w_query: bfloat16 [1024, 1024], replicated, may hold values from -0.1875 to 0.1875
- w_key: bfloat16 [1024, 1024], replicated, may hold values from -0.1875 to 0.1875
- w_value: bfloat16 [1024, 1024], replicated, may hold values from -0.1875 to 0.1875
- w_out: bfloat16 [1024, 1024], replicated, may hold values from -0.1875 to 0.1875
- text_raw: bfloat16 [2048, 1024], P('dp'), may hold values from -0.35 to 0.35
Outputs:
- loss: float32 [], replicated
- text_grad: float32 [2048, 1024], P('dp')
- w_out_grad: bfloat16 [1024, 1024], replicated
All inputs are finite; a program needn't handle non-finite values.
Results may differ from a plain program's by a relative error of at most 0.009.
Values may be sent and summed in bfloat16 or wider, within the bound.
A program may use at most 128 MiB of HBM per device.

v0:
```python
import jax
import jax.numpy as jnp
from jax import lax
from jax.sharding import PartitionSpec as P

HEADS = 16


inv_temp = 1.0 / 0.07
attn_temp = 8.0
epsilon = 1e-06


def side_by_side(arrays, axis, dim, along):
    ends, at = ([], 0)
    for a in arrays[:-1]:
        at += a.shape[along]
        ends.append(at)
    both = jnp.concatenate(arrays, axis=along)
    return tuple(jnp.split(lax.all_gather(both, axis, axis=dim, tiled=True), ends, axis=along))


def layer_norm(inputs, gain):
    center = inputs - jnp.mean(inputs, axis=-1, keepdims=True)
    spread = jnp.mean(center * center, axis=-1, keepdims=True)
    return center * lax.rsqrt(spread + epsilon) * gain


def unit_heads(proj, heads):
    shaped = proj.reshape(proj.shape[0], proj.shape[1], heads, -1)
    return (shaped * lax.rsqrt(jnp.sum(shaped * shaped, axis=-1, keepdims=True) + epsilon)).astype(
        jnp.bfloat16
    )


def embed(feats, ln_gain, w_query, w_key, w_value, w_out):
    images, tokens, width = feats.shape
    inputs = feats.astype(jnp.float32)
    normed = layer_norm(inputs, ln_gain).astype(jnp.bfloat16).reshape(images * tokens, width)
    query = unit_heads(
        jnp.dot(normed, w_query, preferred_element_type=jnp.float32).reshape(images, tokens, width),
        HEADS,
    )
    key_heads = unit_heads(
        jnp.dot(normed, w_key, preferred_element_type=jnp.float32).reshape(images, tokens, width),
        HEADS,
    )
    value_heads = (
        jnp.dot(normed, w_value, preferred_element_type=jnp.float32)
        .reshape(images, tokens, HEADS, -1)
        .astype(jnp.bfloat16)
    )
    scores = attn_temp * jnp.einsum(
        "bqhd,bkhd->bhqk", query, key_heads, preferred_element_type=jnp.float32
    )
    expo = jnp.exp(scores)
    weights = (
        (expo / jnp.sum(expo, axis=-1, keepdims=True)).astype(jnp.bfloat16).astype(jnp.float32)
    )
    pooled = weights[:, :, 0, :] + jnp.mean(weights[:, :, 1:, :], axis=2)
    abar = jnp.einsum(
        "bhk,bkhd->bhd", pooled, value_heads.astype(jnp.float32), precision=lax.Precision.HIGHEST
    )
    abar = abar.reshape(images, width).astype(jnp.bfloat16)
    xbar = inputs[:, 0, :] + jnp.mean(inputs[:, 1:, :], axis=1)
    emb = xbar + jnp.dot(abar, w_out, preferred_element_type=jnp.float32)
    return (emb, abar)


def local(features, ln_gain, w_query, w_key, w_value, w_out, text_raw):
    images = features.shape[0]
    total = images * lax.axis_size("dp")
    offset = lax.axis_index("dp") * images
    text32 = text_raw.astype(jnp.float32)
    txt_norm = jnp.sqrt(jnp.sum(text32 * text32, axis=1, keepdims=True) + epsilon)
    txt_f = text32 / txt_norm
    txt_u = txt_f.astype(jnp.bfloat16)
    emb, abar = embed(features, ln_gain, w_query, w_key, w_value, w_out)
    emb_norm = jnp.sqrt(jnp.sum(emb * emb, axis=1, keepdims=True) + epsilon)
    img_f = emb / emb_norm
    img_u = img_f.astype(jnp.bfloat16)
    row_index = lax.broadcasted_iota(jnp.int32, (images, total), 0)
    col_index = lax.broadcasted_iota(jnp.int32, (images, total), 1)
    diag_mask = jnp.where(col_index == row_index + offset, 1.0, 0.0).astype(jnp.float32)
    all_img, all_txt = side_by_side((img_u, txt_u), "dp", 0, 1)
    logits = inv_temp * jnp.dot(all_img, all_txt.T, preferred_element_type=jnp.float32)
    exp_logits = jnp.exp(logits)
    rowsum = jnp.sum(exp_logits, axis=1)
    colsum = jnp.sum(exp_logits, axis=0)
    diag_logit = jnp.diagonal(logits)
    loss = (jnp.sum(jnp.log(rowsum) - diag_logit) + jnp.sum(jnp.log(colsum) - diag_logit)) / (
        2.0 * total
    )
    row_block = lax.dynamic_slice_in_dim(exp_logits, offset, images, 0)
    own_rowsum = lax.dynamic_slice_in_dim(rowsum, offset, images, 0)
    delta_rows = 0.5 * (row_block / own_rowsum[:, None] + row_block / colsum[None, :]) - diag_mask
    delta_rows = delta_rows.astype(jnp.bfloat16)
    col_block = lax.dynamic_slice_in_dim(exp_logits, offset, images, 1)
    own_colsum = lax.dynamic_slice_in_dim(colsum, offset, images, 0)
    delta_cols = 0.5 * (col_block / rowsum[:, None] + col_block / own_colsum[None, :]) - diag_mask.T
    delta_cols = delta_cols.astype(jnp.bfloat16)
    grad_img = inv_temp * jnp.dot(delta_rows, all_txt, preferred_element_type=jnp.float32)
    grad_txt = inv_temp * lax.dot_general(
        delta_cols, all_img, (((0,), (0,)), ((), ())), preferred_element_type=jnp.float32
    )
    text_grad = (grad_txt - txt_f * jnp.sum(txt_f * grad_txt, axis=1, keepdims=True)) / txt_norm
    emb_grad = (grad_img - img_f * jnp.sum(img_f * grad_img, axis=1, keepdims=True)) / emb_norm
    local_grad = jnp.dot(abar.astype(jnp.float32).T, emb_grad, precision=lax.Precision.HIGHEST)
    w_out_grad = lax.psum(local_grad, "dp").astype(jnp.bfloat16)
    return (loss, text_grad, w_out_grad)


def solution(mesh):
    placed = (P("dp", None, None), P(), P(), P(), P(), P(), P("dp", None))
    return jax.shard_map(
        local, mesh=mesh, in_specs=placed, out_specs=(P(), P("dp", None), P()), check_vma=False
    )
```

profile of v0, /device:TPU:1, one launch (start us, length us, event | category | flops | bytes accessed | tf_op | source)
XLA Modules:
  0.0 401.9 jit_solution(15417415370687040808)
XLA Ops:
  7.2 0.0 copy-start
  7.2 0.0 all-gather.2.cloned.1.call-start
  7.2 4.1 %copy.36 = bf16[1024,1024]{0,1:T(8,128)(2,1)} copy(bf16[1024,1024]{1,0:T(8,128)(2,1)} %param.9) | data formatting | bytes 4194304 | tf_op args[2]
  11.3 0.0 copy-start.5
  11.3 2.8 convert_reduce_fusion
  14.1 2.9 multiply_reduce_fusion.2
  17.0 4.0 copy.38
  20.9 0.0 copy-done.5
  21.0 0.0 copy-start.2
  21.0 3.1 fusion.26
  24.0 0.0 copy-done.2
  24.1 0.0 copy-start.3
  24.1 3.5 multiply_reduce_fusion.1
  27.5 0.0 copy-done.3
  27.6 3.5 multiply_reduce_fusion
  31.1 1.3 fusion.12
  32.4 15.3 %fusion.11 = f32[8,16,128,128]{3,2,1,0:T(8,128)S(1)} fusion(f32[8,16,128,128]{3,2,1,0:T(8,128)S(1)} %fusion.12), kind=kOutput, calls=%fused_computation.24 | output fusion | flops 10502271 | bytes 16777216 | tf_op jit(solution)/shard_map/div | solution.py:58
  47.7 0.1 slice.20
  47.8 0.0 copy-start.1
  47.8 1.9 slice_reduce_fusion
  49.7 0.0 copy-done.1
  49.7 0.0 copy-start.4
  49.7 3.1 copy_convert_fusion
  52.9 0.0 copy-done.4
  52.9 0.1 fusion.33
  53.0 0.1 fusion.56
  53.1 3.9 copy.40
  57.0 7.8 %convolution_convert_fusion = bf16[8,128,16,64]{3,0,2,1:T(8,128)(2,1)S(1)} fusion(bf16[16,64,1024,1]{2,1,0,3:T(8,128)(2,1)} %bitcast.46, f32[1024]{0:T(1024)S(1)} %copy-done.5, f32[8,128]{0,1:T(8,128)S(1)} %add_rsqrt_fusion.2, f32[8,128]{0,1:T(8,128)S(1)} %broadcast_multiply_fusion, bf16[8,128,1024]{2,1,0:T(8,128)(2,1)} %param.7), kind=kOutput, calls=%fused_computation.25 | convolution fusion | flops 2153775104 | bytes 6303744 | tf_op jit(solution)/shard_map/dot_general | solution.py:49
  64.9 7.0 %fusion.2 = f32[8,16,1,64]{3,2,1,0:T(1,128)S(1)} fusion(f32[8,16,128,1]{2,3,1,0:T(1,128)S(1)} %bitcast.47, bf16[8,128,16,64]{3,0,2,1:T(8,128)(2,1)S(1)} %convolution_convert_fusion), kind=kOutput, calls=%fused_computation.7 | convolution fusion | flops 12582912 | bytes 2195456 | tf_op jit(solution)/shard_map/bhk,bkhd->bhd/dot_general | solution.py:61
  71.8 0.1 convert_element_type.55
  71.9 2.5 slice_reduce_fusion.1
  74.4 0.0 copy-done
  74.4 1.3 multiply_reduce_fusion.5
  75.7 0.1 fusion.57
  75.7 0.6 pad_maximum_fusion
  76.4 0.0 all-gather.2.cloned.1.call-update
  76.4 122.1 %all-gather.2.cloned.1.call-done = bf16[2048,2048]{1,0:T(8,128)(2,1)} async-done(((bf16[8,2048]{1,0:T(8,128)(2,1)}), bf16[2048,2048]{1,0:T(8,128)(2,1)}) %all-gather.2.cloned.1.call-update) | async-done | bytes 8388624 | tf_op jit(solution)/shard_map/all_gather | solution.py:20
  198.6 18.7 %exponential_reduce_fusion = (f32[2048]{0:T(1024)S(1)}, f32[2048]{0:T(1024)S(1)}, f32[2048,2048]{0,1:T(8,128)}, f32[2048,2048]{0,1:T(8,128)}) fusion(bf16[2048,2048]{1,0:T(8,128)(2,1)} %all-gather.2.cloned.1.call-done), kind=kOutput, calls=%fused_computation.94 | convolution fusion | flops 8602513408 | bytes 41959424 | tf_op jit(solution)/shard_map/dot_general | solution.py:86
  217.3 0.1 dynamic_slice.13
  217.3 0.1 dynamic_slice.15
  217.4 34.3 %gather_fusion = f32[2048]{0:T(1024)S(1)} fusion(f32[2048,2048]{0,1:T(8,128)} %get-tuple-element.14, s32[2048]{0:T(1024)S(1)} %bitcast.43), kind=kCustom, calls=%fused_computation | custom fusion | bytes 32768 | tf_op jit(solution)/shard_map/jit(diagonal)/cond/branch_0_fun/gather | solution.py:90
  251.7 0.6 subtract_reduce_fusion
  252.3 3.8 multiply_reduce_fusion.3
  256.1 3.8 fusion.35
  259.9 128.9 %all-reduce.1 = bf16[1024,1024]{1,0:T(8,128)(2,1)} all-reduce(f32[1024,1024]{1,0:T(8,128)} %fusion.35), channel_id=1, replica_groups=mesh['dp'=256] {'dp'}, use_global_device_ids=true, to_apply=%region_15.16 | all-reduce | flops 1048576 | bytes 6291456 | tf_op jit(solution)/shard_map/psum | solution.py:109
  390.2 3.0 multiply_reduce_fusion.4
  393.2 0.7 subtract_divide_fusion
  (9 shorter events, 0.1 us)
Async XLA Ops:
  7.2 67.2 %copy-start = (bf16[1024,1024]{1,0:T(8,128)(2,1)S(1)}, bf16[1024,1024]{1,0:T(8,128)(2,1)}, u32[]{:S(2)}) copy-start(bf16[1024,1024]{1,0:T(8,128)(2,1)} %param.12) | copy-start | bytes 6291460
  7.2 191.4 %all-gather.2.cloned.1.call-start = ((), (), s32[]{:S(2)}) async-start(), calls=%async_computation | async-start | bytes 8421376 | tf_op jit(solution)/shard_map/all_gather | solution.py:20
  11.3 9.6 %copy-start.5 = (f32[1024]{0:T(1024)S(1)}, f32[1024]{0:T(1024)}, u32[]{:S(2)}) copy-start(f32[1024]{0:T(1024)} %param.8) | copy-start | bytes 12292
  21.0 3.1 copy-start.2
  24.1 3.5 copy-start.3
  47.8 1.9 copy-start.1
  49.7 3.2 copy-start.4
Sparse Core Ops, SparseCore 0:
  76.5 121.9 all-gather.1
where the time goes:
time: 404 us; the launch traced here: 402 us
  blocking collectives  129 us (32%)
  waiting for transfers between devices  122 us (30%)
  matrix products  53.6 us (13%)
  local copies, waits for them, and re-layouts  46.6 us (12%)
  other arithmetic  33.9 us (8%)
  between operations  16.6 us (4%)
    psum x1, blocking collectives, local(): w_out_grad = lax.psum(local_grad, 'dp').astype(jnp.bfloat16)  129 us
    all_gather x1, waiting for transfers between devices, side_by_side(): lax.all_gather(both, axis, axis=dim, tiled=True)  122 us
    gather x1, local copies, waits for them, and re-layouts, local(): diag_logit = jnp.diagonal(logits)  34.3 us
    dot_general x1, matrix products, local(): jnp.dot(all_img, all_txt.T, preferred_element_type=jnp.float32)  18.7 us
    div x1, other arithmetic, embed(): expo / jnp.sum(expo, axis=-1, keepdims=True)  15.3 us
    unnamed x15, local copies, waits for them, and re-layouts  12 us
  transfers between devices with their start and end apart: 1, of which 1 were waited for; matrix products, arithmetic and copies ran while one was open for 0% of the time, Pallas kernels for 0%

commit v1 on v0

v1 whole, which is shorter than its diff:
```python
import functools

import jax
import jax.numpy as jnp
from jax import lax
from jax.experimental import pallas as pl
from jax.experimental.pallas import tpu as pltpu
from jax.sharding import PartitionSpec as P

INV_TEMP = 1.0 / 0.07
EPS = 1e-06
LOG2E = 1.4426950408889634
F32 = jnp.float32
BF16 = jnp.bfloat16
MESH = pl.DeviceIdType.MESH
NT = (((1,), (1,)), ((), ()))
TN = (((0,), (0,)), ((), ()))
NN = (((1,), (0,)), ((), ()))


def dot(a, b, dims=NN):
    return lax.dot_general(a, b, dims, preferred_element_type=F32)


def iota(shape, dim):
    return lax.broadcasted_iota(jnp.int32, shape, dim)


def embed_kernel(
    feat_hbm, gain_ref, wq_hbm, wk_hbm, wv_hbm, wo_hbm, emb_ref, abar_ref,
    feat, wq, wk, wv, wo, normed, qh, kh, vh, abar, xbar, fsem, wsem,
):
    images = feat.shape[0]
    fcopy = [
        pltpu.make_async_copy(feat_hbm.at[i], feat.at[i], fsem.at[i]) for i in range(images)
    ]
    pairs = ((wq_hbm, wq), (wk_hbm, wk), (wv_hbm, wv), (wo_hbm, wo))
    wcopy = [pltpu.make_async_copy(s, d, wsem.at[i]) for i, (s, d) in enumerate(pairs)]
    for cp in fcopy + wcopy:
        cp.start()
    gain = gain_ref[...]

    for i in range(images):
        fcopy[i].wait()

        def norm_rows(t, total, i=i):
            rows = pl.ds(pl.multiple_of(t * 32, 32), 32)
            x = feat[i, rows, :].astype(F32)
            center = x - jnp.mean(x, axis=-1, keepdims=True)
            spread = jnp.mean(center * center, axis=-1, keepdims=True)
            out = center * lax.rsqrt(spread + EPS) * gain
            normed[pl.ds(pl.multiple_of(i * 128 + t * 32, 32), 32), :] = out.astype(BF16)
            return total + jnp.sum(x.reshape(4, 8, 1024), axis=0)

        total = lax.fori_loop(0, 4, norm_rows, jnp.zeros((8, 1024), F32))
        total = jnp.sum(total, axis=0, keepdims=True)
        first = feat[i, 0:16, :].astype(F32)[0:1]
        xbar[i : i + 1, :] = first + (total - first) * (1.0 / 127.0)

    same_head = jnp.where(
        iota((256, 256), 0) // 64 == iota((256, 256), 1) // 64, 1.0, 0.0
    ).astype(BF16)

    def project(w, out, scale):
        def step(t, carry):
            rows = pl.ds(pl.multiple_of((t % 2) * 512, 512), 512)
            cols = pl.ds(pl.multiple_of((t // 2) * 256, 256), 256)
            proj = dot(normed[rows, :], w[:, cols])
            if scale is not None:
                squares = dot((proj * proj).astype(BF16), same_head)
                proj = proj * (lax.rsqrt(squares + EPS) * scale)
            out[rows, cols] = proj.astype(BF16)
            return carry

        lax.fori_loop(0, 8, step, 0)

    wcopy[0].wait()
    project(wq, qh, 8.0 * LOG2E)
    wcopy[1].wait()
    project(wk, kh, 1.0)
    wcopy[2].wait()
    project(wv, vh, None)

    lane = iota((1, 128), 1)
    low = jnp.where(lane < 64, 1.0, 0.0).astype(BF16)
    high = jnp.where(lane < 64, 0.0, 1.0).astype(BF16)
    share = jnp.where(iota((1, 256), 1) % 128 == 0, 1.0, 1.0 / 127.0).astype(F32)
    gather = jnp.where(
        iota((256, 128), 0) // 128 == iota((256, 128), 1) // 64, 1.0, 0.0
    ).astype(BF16)

    def attend(i, carry):
        rows = pl.ds(pl.multiple_of(i * 128, 128), 128)
        parts = []
        for p in range(8):
            cols = slice(p * 128, p * 128 + 128)
            q = qh[rows, cols]
            both = jnp.concatenate([q * low, q * high], axis=0)
            expo = jnp.exp2(dot(kh[rows, cols], both, NT))
            weight = share / jnp.sum(expo, axis=0, keepdims=True)
            pooled = dot((expo * weight).astype(BF16), gather)
            parts.append(jnp.sum(pooled * vh[rows, cols].astype(F32), axis=0, keepdims=True))
        abar[pl.ds(i, 1), :] = jnp.concatenate(parts, axis=1)
        return carry

    lax.fori_loop(0, images, attend, 0)
    rounded = abar[...].astype(BF16)
    abar_ref[...] = abar[...]
    wcopy[3].wait()
    emb_ref[...] = xbar[...] + dot(rounded, wo[...])


def embed(features, gain, wq, wk, wv, wo):
    images, tokens, width = features.shape
    rows = images * tokens
    any_spec = pl.BlockSpec(memory_space=pl.ANY)
    vmem = pl.BlockSpec(memory_space=pltpu.VMEM)
    square = pltpu.VMEM((width, width), BF16)
    return pl.pallas_call(
        embed_kernel,
        out_shape=[
            jax.ShapeDtypeStruct((images, width), F32),
            jax.ShapeDtypeStruct((images, width), F32),
        ],
        in_specs=[any_spec, vmem, any_spec, any_spec, any_spec, any_spec],
        out_specs=[vmem, vmem],
        scratch_shapes=[
            pltpu.VMEM((images, tokens, width), BF16),
            square, square, square, square,
            pltpu.VMEM((rows, width), BF16),
            pltpu.VMEM((rows, width), BF16),
            pltpu.VMEM((rows, width), BF16),
            pltpu.VMEM((rows, width), BF16),
            pltpu.VMEM((images, width), F32),
            pltpu.VMEM((images, width), F32),
            pltpu.SemaphoreType.DMA((images,)),
            pltpu.SemaphoreType.DMA((4,)),
        ],
        compiler_params=pltpu.CompilerParams(vmem_limit_bytes=48 << 20),
        name="embed",
    )(features, gain, wq, wk, wv, wo)


def pack_rows(col):
    lane = iota((8, 128), 1)
    tile = jnp.zeros((8, 128), F32)
    for k in range(8):
        tile = jnp.where(lane == k, col[8 * k : 8 * k + 8], tile)
    return tile


def unpack_rows(tile):
    return jnp.concatenate([tile[:, k : k + 1] for k in range(8)], axis=0)


def loss_kernel(
    emb_ref, abar_ref, text_ref, wgrad, tgrad_ref, loss_ref,
    t_all, u_all, a_all, rs_all, cs_all, g_send, g_recv, s_all,
    h_send, h_recv, w_send, w_recv, l_all, send, recv, c1, c2,
):
    idx = lax.axis_index("dp")
    core = idx % 2
    z = (idx // 2) % 8
    x = (idx // 16) % 4
    y = idx // 64
    c = x * 2 + core
    r = y * 8 + z

    def row_peer(k):
        p = (c + k) % 8
        return p, (y * 64 + (p // 2) * 16 + z * 2 + p % 2,)

    def col_peer(k):
        p = (r + k) % 32
        return p, ((p // 8) * 64 + x * 16 + (p % 8) * 2 + core,)

    a = y * (1 - core) + x * core
    b = x * (1 - core) + y * core

    def place(a1, b1):
        y1 = a1 * (1 - core) + b1 * core
        x1 = b1 * (1 - core) + a1 * core
        return y1, x1

    def device(a1, b1, z1, core1):
        y1, x1 = place(a1, b1)
        return (y1 * 64 + x1 * 16 + z1 * 2 + core1,)

    def plane_peer(k):
        p = (a * 8 + z + k) % 32
        return p, device(p // 8, b, p % 8, core)

    barrier = pltpu.get_barrier_semaphore()

    def greet(peer):
        def step(k, carry):
            pl.semaphore_signal(barrier, inc=1, device_id=peer(k)[1], device_id_type=MESH)
            return carry

        return step

    lax.fori_loop(1, 8, greet(row_peer), 0)
    lax.fori_loop(1, 32, greet(col_peer), 0)
    lax.fori_loop(1, 32, greet(plane_peer), 0)

    def push(src, dst, s, dev):
        pltpu.make_async_remote_copy(
            src_ref=src, dst_ref=dst, send_sem=send.at[s], recv_sem=recv.at[s],
            device_id=dev, device_id_type=MESH,
        ).start()

    def share(buf, slot, s, peer, n):
        def step(k, carry):
            push(buf.at[slot], buf.at[slot], s, peer(k)[1])
            return carry

        lax.fori_loop(1, n, step, 0)

    def scatter(src, dst, slot, s, peer, n):
        def step(k, carry):
            p, dev = peer(k)
            push(src.at[p], dst.at[slot], s, dev)
            return carry

        lax.fori_loop(1, n, step, 0)

    def local(src, dst, sem):
        return pltpu.make_async_copy(src, dst, sem)

    def arrived(buf, s, n):
        part = buf.at[pl.ds(0, n - 1)]
        local(part, part, recv.at[s]).wait()

    def left(buf, s, n):
        part = buf.at[pl.ds(0, n - 1)]
        local(part, part, send.at[s]).wait()

    text = text_ref[...].astype(F32)
    txt_norm = jnp.sqrt(jnp.sum(text * text, axis=1, keepdims=True) + EPS)
    txt_f = text / txt_norm
    txt_u = txt_f.astype(BF16)
    t_all[r] = txt_u
    emb = emb_ref[...]
    emb_norm = jnp.sqrt(jnp.sum(emb * emb, axis=1, keepdims=True) + EPS)
    img_u = (emb / emb_norm).astype(BF16)
    u_all[c] = img_u
    abar = abar_ref[...].astype(BF16).astype(F32)
    a_all[c] = (abar / emb_norm).astype(BF16)
    diag = INV_TEMP * jnp.sum(
        jnp.sum(img_u.astype(F32) * txt_u.astype(F32), axis=1, keepdims=True),
        axis=0, keepdims=True,
    )

    pl.semaphore_wait(barrier, 7 + 31 + 31)
    share(u_all, c, 0, row_peer, 8)
    share(t_all, r, 1, col_peer, 32)
    share(a_all, c, 2, row_peer, 8)

    arrived(u_all, 0, 8)
    arrived(t_all, 1, 32)
    img = u_all[...].astype(F32).reshape(64, 1024).astype(BF16)
    txt = t_all[...].astype(F32).reshape(256, 1024).astype(BF16)
    logits = INV_TEMP * dot(img, txt, NT)
    expo = jnp.exp(logits)
    cs_all[r] = jnp.sum(expo, axis=0, keepdims=True)
    share(cs_all, r, 3, col_peer, 32)
    rs_all[c] = pack_rows(jnp.sum(expo, axis=1, keepdims=True))
    share(rs_all, c, 4, row_peer, 8)
    arrived(rs_all, 4, 8)
    arrived(cs_all, 3, 32)

    row_tile = jnp.sum(rs_all[...], axis=0)
    rowsum = unpack_rows(row_tile)
    colsum = jnp.sum(cs_all[...], axis=0)
    probs = expo * (0.5 / rowsum + 0.5 / colsum)
    row = iota((64, 256), 0) - c * 8
    col = iota((64, 256), 1) - r * 8
    same = (row == col) & (row >= 0) & (row < 8)
    delta = (probs - jnp.where(same, 1.0, 0.0)).astype(BF16)
    s_part = jnp.sum(delta.astype(F32) * logits, axis=1, keepdims=True)
    own_rows = jnp.where(iota((8, 128), 1) == c, jnp.log(row_tile), 0.0)
    own = iota((1, 256), 1) - r * 8
    own_cols = jnp.where((own >= 0) & (own < 8), jnp.log(colsum), 0.0)
    loss = (
        jnp.sum(jnp.sum(own_rows, axis=1, keepdims=True), axis=0, keepdims=True)
        + jnp.sum(own_cols, axis=1, keepdims=True)
        - 2.0 * diag
    )
    s_tile = pack_rows(s_part)
    s_all[c] = jnp.where(iota((8, 128), 1) == 8, loss, s_tile)
    share(s_all, c, 5, row_peer, 8)
    grad = INV_TEMP * dot(delta, txt)
    for k in range(8):
        g_send[k] = grad[:, 128 * k : 128 * k + 128].astype(BF16)
    g_recv[c] = g_send[c]
    scatter(g_send, g_recv, c, 6, row_peer, 8)

    part = INV_TEMP * dot(probs.astype(BF16), img, TN)
    h_send[...] = part.astype(BF16).astype(F32).reshape(32, 8, 1024).astype(BF16)
    h_recv[r] = h_send[r]
    scatter(h_send, h_recv, r, 7, col_peer, 32)

    arrived(s_all, 5, 8)
    arrived(g_recv, 6, 8)
    arrived(a_all, 2, 8)
    s_sum = jnp.sum(s_all[...], axis=0)
    my_cols = pl.ds(pl.multiple_of(c * 128, 128), 128)
    f_cols = u_all[:, :, my_cols].astype(F32).reshape(64, 128)
    g_sum = jnp.sum(g_recv[...].astype(F32), axis=0)
    emb_grad = (g_sum - f_cols * unpack_rows(s_sum)).astype(BF16)
    scaled = a_all[...].astype(F32).reshape(64, 1024).astype(BF16)
    w_send[...] = dot(scaled, emb_grad, TN).astype(BF16).reshape(32, 32, 128)
    w_recv[r] = w_send[r]
    scatter(w_send, w_recv, r, 8, col_peer, 32)
    l_all[r] = jnp.sum(jnp.where(iota((8, 128), 1) == 8, s_sum, 0.0), axis=0, keepdims=True) * 0.125
    share(l_all, r, 9, col_peer, 32)

    arrived(w_recv, 8, 32)
    block = jnp.sum(w_recv[...].astype(F32), axis=0).astype(BF16)

    def chunk(a1, b1, core1):
        y1, x1 = place(a1, b1)
        return wgrad.at[
            pl.ds(pl.multiple_of(y1 * 256, 256), 256),
            pl.ds(pl.multiple_of((x1 * 2 + core1) * 128, 128), 128),
        ]

    mine = wgrad.at[pl.ds(pl.multiple_of(r * 32, 32), 32), my_cols]
    mine[...] = block

    def first(k, carry):
        pltpu.make_async_remote_copy(
            src_ref=mine, dst_ref=mine, send_sem=send.at[10], recv_sem=c1.at[a],
            device_id=plane_peer(k)[1], device_id_type=MESH,
        ).start()
        return carry

    lax.fori_loop(1, 32, first, 0)

    arrived(h_recv, 7, 32)
    g_txt = jnp.sum(h_recv[...].astype(F32), axis=0) - INV_TEMP * img_u.astype(F32)
    tgrad_ref[...] = (
        g_txt - txt_f * jnp.sum(txt_f * g_txt, axis=1, keepdims=True)
    ) / txt_norm
    arrived(l_all, 9, 32)
    total = jnp.sum(jnp.sum(l_all[...], axis=0), axis=1, keepdims=True)
    loss_ref[...] = jnp.broadcast_to(total * (1.0 / 4096.0), (1, 128))

    def second(j, carry):
        a1 = (a + j) % 4
        piece = chunk(a1, b, core)

        @pl.when(j == 0)
        def _():
            short = wgrad.at[pl.ds(0, 224), pl.ds(0, 128)]
            local(short, short, c1.at[a]).wait()

        @pl.when(j > 0)
        def _():
            local(piece, piece, c1.at[a1]).wait()

        for m in range(1, 4):
            pltpu.make_async_remote_copy(
                src_ref=piece, dst_ref=piece, send_sem=send.at[11],
                recv_sem=c2.at[b * 4 + a1],
                device_id=device(a, (b + m) % 4, z, core), device_id_type=MESH,
            ).start()
        pltpu.make_async_remote_copy(
            src_ref=piece, dst_ref=piece, send_sem=send.at[11], recv_sem=recv.at[10],
            device_id=(idx + 1 - 2 * core,), device_id_type=MESH,
        ).start()
        return carry

    lax.fori_loop(0, 4, second, 0)

    def third(t, carry):
        a1 = (a + t // 3) % 4
        b1 = (b + 1 + t % 3) % 4
        piece = chunk(a1, b1, core)
        local(piece, piece, c2.at[b1 * 4 + a1]).wait()
        pltpu.make_async_remote_copy(
            src_ref=piece, dst_ref=piece, send_sem=send.at[11], recv_sem=recv.at[10],
            device_id=(idx + 1 - 2 * core,), device_id_type=MESH,
        ).start()
        return carry

    lax.fori_loop(0, 12, third, 0)
    half = wgrad.at[:, pl.ds(0, 512)]
    local(half, half, recv.at[10]).wait()

    left(u_all, 0, 8)
    left(t_all, 1, 32)
    left(a_all, 2, 8)
    left(cs_all, 3, 32)
    left(rs_all, 4, 8)
    left(s_all, 5, 8)
    left(g_send, 6, 8)
    left(h_send, 7, 32)
    left(w_send, 8, 32)
    left(l_all, 9, 32)
    tall = wgrad.at[pl.ds(0, 992), pl.ds(0, 128)]
    local(tall, tall, send.at[10]).wait()
    wide = wgrad.at[:, pl.ds(0, 896)]
    local(wide, wide, send.at[11]).wait()


def contrast(emb, abar, text):
    images, width = emb.shape
    vmem = pl.BlockSpec(memory_space=pltpu.VMEM)
    return pl.pallas_call(
        loss_kernel,
        out_shape=[
            jax.ShapeDtypeStruct((width, width), BF16),
            jax.ShapeDtypeStruct((images, width), F32),
            jax.ShapeDtypeStruct((1, 128), F32),
        ],
        in_specs=[vmem, vmem, vmem],
        out_specs=[vmem, vmem, vmem],
        scratch_shapes=[
            pltpu.VMEM((32, 8, width), BF16),
            pltpu.VMEM((8, 8, width), BF16),
            pltpu.VMEM((8, 8, width), BF16),
            pltpu.VMEM((8, 8, 128), F32),
            pltpu.VMEM((32, 1, 256), F32),
            pltpu.VMEM((8, 64, 128), BF16),
            pltpu.VMEM((8, 64, 128), BF16),
            pltpu.VMEM((8, 8, 128), F32),
            pltpu.VMEM((32, 8, width), BF16),
            pltpu.VMEM((32, 8, width), BF16),
            pltpu.VMEM((32, 32, 128), BF16),
            pltpu.VMEM((32, 32, 128), BF16),
            pltpu.VMEM((32, 1, 128), F32),
            pltpu.SemaphoreType.DMA((12,)),
            pltpu.SemaphoreType.DMA((11,)),
            pltpu.SemaphoreType.DMA((4,)),
            pltpu.SemaphoreType.DMA((16,)),
        ],
        compiler_params=pltpu.CompilerParams(
            collective_id=0, has_side_effects=True, vmem_limit_bytes=40 << 20
        ),
        name="contrast",
    )(emb, abar, text)


def local(features, ln_gain, w_query, w_key, w_value, w_out, text_raw):
    emb, abar = embed(features, ln_gain.reshape(1, -1), w_query, w_key, w_value, w_out)
    wgrad, tgrad, loss = contrast(emb, abar, text_raw)
    return (loss[0, 0], tgrad, wgrad)


def solution(mesh):
    placed = (P("dp", None, None), P(), P(), P(), P(), P(), P("dp", None))
    return jax.shard_map(
        local, mesh=mesh, in_specs=placed, out_specs=(P(), P("dp", None), P()), check_vma=False
    )
```

time: 404 us -> 107 us (0.26)
  blocking collectives: 129 us -> 0 us
  waiting for transfers between devices: 122 us -> 0 us
  Pallas kernels: 0 us -> 99.1 us
  matrix products: 53.6 us -> 0 us
  local copies, waits for them, and re-layouts: 46.6 us -> 5.8 us
  other arithmetic: 33.9 us -> 0 us
  between operations: 16.6 us -> 1.83 us
    psum x1 -> x0, blocking collectives: 129 us -> none  [local(): w_out_grad = lax.psum(local_grad, 'dp').astype(jnp.bfloat16)]
    all_gather x1 -> x0, waiting for transfers between devices: 122 us -> none  [side_by_side(): lax.all_gather(both, axis, axis=dim, tiled=True)]
    pallas_call x0 -> x2, Pallas kernels: none -> 99.1 us  [the longest x1 71.5 us: contrast(): pl.pallas_call(loss_kernel, out_shape=[jax.ShapeDtypeStruct((width, width...]
    dot_general x10 -> x0, matrix products: 53.6 us -> none  [the longest x1 18.7 us: local(): jnp.dot(all_img, all_txt.T, preferred_element_type=jnp.float32)]
    gather x1 -> x0, local copies, waits for them, and re-layouts: 34.3 us -> none  [local(): diag_logit = jnp.diagonal(logits)]
    div x3 -> x0, other arithmetic: 16 us -> none  [the longest x1 15.3 us: embed(): expo / jnp.sum(expo, axis=-1, keepdims=True)]
    reduce_sum x6 -> x0, other arithmetic: 10.8 us -> none  [the longest x1 2.86 us: layer_norm(): spread = jnp.mean(center * center, axis=-1, keepdims=True)]
    convert_element_type x5 -> x0, other arithmetic: 6.4 us -> none  [the longest x1 3.14 us: embed(): inputs = feats.astype(jnp.float32)]
  transfers between devices with their start and end apart: 1 -> 0, of which waited for: 1 -> 0; matrix products, arithmetic and copies ran while one was open for 0% -> 0% of each run, Pallas kernels for 0% -> 0%
where the time goes in v1:
time: 107 us
  Pallas kernels  99.1 us (93%)
  local copies, waits for them, and re-layouts  5.8 us (5%)
  between operations  1.83 us (2%)
    pallas_call x1, Pallas kernels, contrast(): pl.pallas_call(loss_kernel, out_shape=[jax.ShapeDtypeStruct((width, width...  71.5 us
    pallas_call x1, Pallas kernels, embed(): pl.pallas_call(embed_kernel, out_shape=[jax.ShapeDtypeStruct((images, wid...  27.6 us
    unnamed x10, local copies, waits for them, and re-layouts  5.8 us

profile of v1, /device:TPU:1, one launch (start us, length us, event | category | flops | bytes accessed | tf_op | source)
XLA Modules:
  0.0 106.7 jit_solution(10967543067551332995)
XLA Ops:
  0.6 0.0 copy-start
  0.6 1.6 %copy-done = bf16[8,128,1024]{2,1,0:T(8,128)(2,1)S(1)} copy-done((bf16[8,128,1024]{2,1,0:T(8,128)(2,1)S(1)}, bf16[8,128,1024]{2,1,0:T(8,128)(2,1)}, u32[]{:S(2)}) %copy-start) | copy-done | bytes 2097176
  2.2 0.0 copy-start.1
  2.2 1.6 %copy-done.1 = bf16[1024,1024]{1,0:T(8,128)(2,1)S(1)} copy-done((bf16[1024,1024]{1,0:T(8,128)(2,1)S(1)}, bf16[1024,1024]{1,0:T(8,128)(2,1)}, u32[]{:S(2)}) %copy-start.1) | copy-done | bytes 2097176
  3.8 0.0 copy-start.3
  3.8 0.7 copy-done.3
  4.5 0.0 copy-start.2
  4.5 27.6 %embed.1 = (f32[8,1024]{1,0:T(8,128)S(1)}, f32[8,1024]{1,0:T(8,128)S(1)}) custom-call(bf16[8,128,1024]{2,1,0:T(8,128)(2,1)S(1)} %copy-done, f32[1,1024]{1,0:T(1,128)S(1)} %bitcast.3, bf16[1024,1024]{1,0:T(8,128)(2,1)S(1)} %copy-done.1, bf16[1024,1024]{1,0:T(8,128)(2,1)} %wk_hbm.1, bf16[1024,1024]{1,0:T(8,128)(2,1)} %wv_hbm.1, bf16[1024,1024]{1,0:T(8,128)(2,1)} %wo_hbm.1), custom_call_target="tpu_custom_call" | custom-call | tf_op jit(solution)/shard_map/embed/pallas_call | solution.py:119
  32.1 0.0 copy-done.2
  32.1 71.5 %contrast.1 = (bf16[1024,1024]{1,0:T(8,128)(2,1)S(1)}, f32[8,1024]{1,0:T(8,128)S(1)}, f32[1,128]{1,0:T(1,128)S(1)}) custom-call(f32[8,1024]{1,0:T(8,128)S(1)} %get-tuple-element.8.emb_ref, f32[8,1024]{1,0:T(8,128)S(1)} %get-tuple-element.9.abar_ref, bf16[8,1024]{1,0:T(8,128)(2,1)S(1)} %copy-done.2), custom_call_target="tpu_custom_call" | custom-call | tf_op jit(solution)/shard_map/contrast/pallas_call | solution.py:410
  103.7 0.6 copy.14
  104.3 1.3 %copy.15 = bf16[1024,1024]{1,0:T(8,128)(2,1)} copy(bf16[1024,1024]{1,0:T(8,128)(2,1)S(1)} %get-tuple-element.18) | data formatting | bytes 4194304
Async XLA Ops:
  0.6 1.6 %copy-start = (bf16[8,128,1024]{2,1,0:T(8,128)(2,1)S(1)}, bf16[8,128,1024]{2,1,0:T(8,128)(2,1)}, u32[]{:S(2)}) copy-start(bf16[8,128,1024]{2,1,0:T(8,128)(2,1)} %feat_hbm.1) | copy-start | bytes 6291460
  2.2 1.6 %copy-start.1 = (bf16[1024,1024]{1,0:T(8,128)(2,1)S(1)}, bf16[1024,1024]{1,0:T(8,128)(2,1)}, u32[]{:S(2)}) copy-start(bf16[1024,1024]{1,0:T(8,128)(2,1)} %wq_hbm.1) | copy-start | bytes 6291460
  3.8 0.7 copy-start.3
  4.5 27.6 %copy-start.2 = (bf16[8,1024]{1,0:T(8,128)(2,1)S(1)}, bf16[8,1024]{1,0:T(8,128)(2,1)}, u32[]{:S(2)}) copy-start(bf16[8,1024]{1,0:T(8,128)(2,1)} %text_ref.1) | copy-start | bytes 49156

commit v2 on v1

v2 whole, which is shorter than its diff:
```python
import jax
import jax.numpy as jnp
from jax import lax
from jax.experimental import pallas as pl
from jax.experimental.pallas import tpu as pltpu
from jax.sharding import PartitionSpec as P

INV_TEMP = 1.0 / 0.07
EPS = 1e-06
LOG2E = 1.4426950408889634
F32 = jnp.float32
BF16 = jnp.bfloat16
MESH = pl.DeviceIdType.MESH
NT = (((1,), (1,)), ((), ()))
TN = (((0,), (0,)), ((), ()))
NN = (((1,), (0,)), ((), ()))


def dot(a, b, dims=NN):
    return lax.dot_general(a, b, dims, preferred_element_type=F32)


def iota(shape, dim):
    return lax.broadcasted_iota(jnp.int32, shape, dim)


def pack_rows(col):
    lane = iota((8, 128), 1)
    tile = jnp.zeros((8, 128), F32)
    for k in range(8):
        tile = jnp.where(lane == k, col[8 * k : 8 * k + 8], tile)
    return tile


def unpack_rows(tile):
    return jnp.concatenate([tile[:, k : k + 1] for k in range(8)], axis=0)


def rows_of(ref):
    n, eight, width = ref.shape
    return ref[...].astype(F32).reshape(n * eight, width).astype(BF16)


def step_kernel(
    feat_hbm, gain_ref, wq_hbm, wk_hbm, wv_hbm, wo_hbm, text_ref,
    wgrad, tgrad_ref, loss_ref,
    feat, wq, wk, wv, wo, normed, qh, kh, vh, abar_f, xbar, fsem, wsem,
    t_all, t_row, u_all, u_col, a_all, rs_all, cs_all, rg_all, cg_all,
    g_send, g_recv, s_all, h_send, h_recv, w_send, w_recv, l_all, send, recv, c1, c2,
):
    idx = lax.axis_index("dp")
    core = idx % 2
    z = (idx // 2) % 8
    x = (idx // 16) % 4
    y = idx // 64
    c = x * 2 + core
    r = y * 8 + z

    def row_peer(k):
        p = (c + k) % 8
        return p, (y * 64 + (p // 2) * 16 + z * 2 + p % 2,)

    def col_peer(k):
        p = (r + k) % 32
        return p, ((p // 8) * 64 + x * 16 + (p % 8) * 2 + core,)

    a = y * (1 - core) + x * core
    b = x * (1 - core) + y * core

    def place(a1, b1):
        y1 = a1 * (1 - core) + b1 * core
        x1 = b1 * (1 - core) + a1 * core
        return y1, x1

    def device(a1, b1, z1, core1):
        y1, x1 = place(a1, b1)
        return (y1 * 64 + x1 * 16 + z1 * 2 + core1,)

    def plane_peer(k):
        p = (a * 8 + z + k) % 32
        return p, device(p // 8, b, p % 8, core)

    images = feat.shape[0]
    fcopy = [
        pltpu.make_async_copy(feat_hbm.at[i], feat.at[i], fsem.at[i]) for i in range(images)
    ]
    pairs = ((wq_hbm, wq), (wk_hbm, wk), (wv_hbm, wv), (wo_hbm, wo))
    wcopy = [pltpu.make_async_copy(s, d, wsem.at[i]) for i, (s, d) in enumerate(pairs)]
    for cp in fcopy + wcopy:
        cp.start()

    barrier = pltpu.get_barrier_semaphore()

    def greet(peer):
        def step(k, carry):
            pl.semaphore_signal(barrier, inc=1, device_id=peer(k)[1], device_id_type=MESH)
            return carry

        return step

    lax.fori_loop(1, 8, greet(row_peer), 0)
    lax.fori_loop(1, 32, greet(col_peer), 0)
    lax.fori_loop(1, 32, greet(plane_peer), 0)

    def push(src, dst, s, dev):
        pltpu.make_async_remote_copy(
            src_ref=src, dst_ref=dst, send_sem=send.at[s], recv_sem=recv.at[s],
            device_id=dev, device_id_type=MESH,
        ).start()

    def share(buf, slot, s, peer, n):
        def step(k, carry):
            push(buf.at[slot], buf.at[slot], s, peer(k)[1])
            return carry

        lax.fori_loop(1, n, step, 0)

    def scatter(src, dst, slot, s, peer, n):
        def step(k, carry):
            p, dev = peer(k)
            push(src.at[p], dst.at[slot], s, dev)
            return carry

        lax.fori_loop(1, n, step, 0)

    def local(src, dst, sem):
        return pltpu.make_async_copy(src, dst, sem)

    def arrived(buf, s, n):
        part = buf.at[pl.ds(0, n - 1)]
        local(part, part, recv.at[s]).wait()

    def left(buf, s, n):
        part = buf.at[pl.ds(0, n - 1)]
        local(part, part, send.at[s]).wait()

    text = text_ref[...].astype(F32)
    txt_norm = jnp.sqrt(jnp.sum(text * text, axis=1, keepdims=True) + EPS)
    txt_f = text / txt_norm
    txt_u = txt_f.astype(BF16)
    t_all[r] = txt_u
    t_row[c] = txt_u
    gain = gain_ref[...]

    with jax.named_scope("norm"):
        for i in range(images):
            fcopy[i].wait()

            def norm_rows(t, total, i=i):
                rows = pl.ds(pl.multiple_of(t * 32, 32), 32)
                x = feat[i, rows, :].astype(F32)
                center = x - jnp.mean(x, axis=-1, keepdims=True)
                spread = jnp.mean(center * center, axis=-1, keepdims=True)
                out = center * lax.rsqrt(spread + EPS) * gain
                normed[pl.ds(pl.multiple_of(i * 128 + t * 32, 32), 32), :] = out.astype(BF16)
                return total + jnp.sum(x.reshape(4, 8, 1024), axis=0)

            total = lax.fori_loop(0, 4, norm_rows, jnp.zeros((8, 1024), F32))
            total = jnp.sum(total, axis=0, keepdims=True)
            first = feat[i, 0:16, :].astype(F32)[0:1]
            xbar[i : i + 1, :] = first + (total - first) * (1.0 / 127.0)

    with jax.named_scope("greet"):
        pl.semaphore_wait(barrier, 7 + 31 + 31)
        share(t_all, r, 1, col_peer, 32)
        share(t_row, c, 12, row_peer, 8)

    same_head = jnp.where(
        iota((256, 256), 0) // 64 == iota((256, 256), 1) // 64, 1.0, 0.0
    ).astype(BF16)

    def project(w, out, scale):
        def step(t, carry):
            rows = pl.ds(pl.multiple_of((t % 2) * 512, 512), 512)
            cols = pl.ds(pl.multiple_of((t // 2) * 256, 256), 256)
            proj = dot(normed[rows, :], w[:, cols])
            if scale is not None:
                squares = dot((proj * proj).astype(BF16), same_head)
                proj = proj * (lax.rsqrt(squares + EPS) * scale)
            out[rows, cols] = proj.astype(BF16)
            return carry

        lax.fori_loop(0, 8, step, 0)

    with jax.named_scope("query"):
        wcopy[0].wait()
        project(wq, qh, 8.0 * LOG2E)
    with jax.named_scope("key"):
        wcopy[1].wait()
        project(wk, kh, 1.0)
    with jax.named_scope("value"):
        wcopy[2].wait()
        project(wv, vh, None)

    lane = iota((1, 128), 1)
    low = jnp.where(lane < 64, 1.0, 0.0).astype(BF16)
    high = jnp.where(lane < 64, 0.0, 1.0).astype(BF16)
    weigh = jnp.where(iota((1, 256), 1) % 128 == 0, 1.0, 1.0 / 127.0).astype(F32)
    gather = jnp.where(
        iota((256, 128), 0) // 128 == iota((256, 128), 1) // 64, 1.0, 0.0
    ).astype(BF16)

    def attend(i, carry):
        rows = pl.ds(pl.multiple_of(i * 128, 128), 128)
        parts = []
        for p in range(8):
            cols = slice(p * 128, p * 128 + 128)
            q = qh[rows, cols]
            both = jnp.concatenate([q * low, q * high], axis=0)
            expo = jnp.exp2(dot(kh[rows, cols], both, NT))
            weight = weigh / jnp.sum(expo, axis=0, keepdims=True)
            pooled = dot((expo * weight).astype(BF16), gather)
            parts.append(jnp.sum(pooled * vh[rows, cols].astype(F32), axis=0, keepdims=True))
        abar_f[pl.ds(i, 1), :] = jnp.concatenate(parts, axis=1)
        return carry

    with jax.named_scope("attend"):
        lax.fori_loop(0, images, attend, 0)

    with jax.named_scope("emb"):
        abar = abar_f[...].astype(BF16)
        wcopy[3].wait()
        emb = xbar[...] + dot(abar, wo[...])
        emb_norm = jnp.sqrt(jnp.sum(emb * emb, axis=1, keepdims=True) + EPS)
        img_u = (emb / emb_norm).astype(BF16)
        u_all[c] = img_u
        u_col[r] = img_u
        a_all[c] = (abar.astype(F32) / emb_norm).astype(BF16)
        share(u_all, c, 0, row_peer, 8)
        share(a_all, c, 2, row_peer, 8)
        diag = INV_TEMP * jnp.sum(
            jnp.sum(img_u.astype(F32) * txt_u.astype(F32), axis=1, keepdims=True),
            axis=0, keepdims=True,
        )

    with jax.named_scope("wait_text"):
        arrived(t_all, 1, 32)
    with jax.named_scope("wait_img"):
        arrived(u_all, 0, 8)
    with jax.named_scope("logits"):
        img = rows_of(u_all)
        txt = rows_of(t_all)
        logits = INV_TEMP * dot(img, txt, NT)
        expo = jnp.exp(logits)
        cs_all[r] = jnp.sum(expo, axis=0, keepdims=True)
        share(cs_all, r, 3, col_peer, 32)
        rs_all[c] = pack_rows(jnp.sum(expo, axis=1, keepdims=True))
        share(rs_all, c, 4, row_peer, 8)
        share(u_col, r, 13, col_peer, 32)
    with jax.named_scope("wait_sums"):
        arrived(rs_all, 4, 8)
        arrived(cs_all, 3, 32)

    with jax.named_scope("delta"):
        row_tile = jnp.sum(rs_all[...], axis=0)
        colsum = jnp.sum(cs_all[...], axis=0)
        probs = expo * (0.5 / unpack_rows(row_tile) + 0.5 / colsum)
        row = iota((64, 256), 0) - c * 8
        col = iota((64, 256), 1) - r * 8
        same = (row == col) & (row >= 0) & (row < 8)
        delta = (probs - jnp.where(same, 1.0, 0.0)).astype(BF16)
        grad = INV_TEMP * dot(delta, txt)
        for k in range(8):
            g_send[k] = grad[:, 128 * k : 128 * k + 128].astype(BF16)
        g_recv[c] = g_send[c]
        scatter(g_send, g_recv, c, 6, row_peer, 8)
        s_part = jnp.sum(delta.astype(F32) * logits, axis=1, keepdims=True)
        my_lane = iota((8, 128), 1) == c
        own_rows = jnp.where(my_lane, row_tile, 0.0)
        own = iota((1, 256), 1) - r * 8
        own_cols = jnp.where((own >= 0) & (own < 8), colsum, 0.0)
        loss = (
            jnp.sum(
                jnp.sum(jnp.log(jnp.where(my_lane, row_tile, 1.0)), axis=1, keepdims=True),
                axis=0, keepdims=True,
            )
            + jnp.sum(
                jnp.log(jnp.where((own >= 0) & (own < 8), colsum, 1.0)), axis=1, keepdims=True
            )
            - 2.0 * diag
        )
        s_all[c] = jnp.where(iota((8, 128), 1) == 8, loss, pack_rows(s_part))
        share(s_all, c, 5, row_peer, 8)
        own_row = jnp.sum(own_rows, axis=1, keepdims=True)
        spot = iota((8, 256), 1) - r * 8 == iota((8, 256), 0)
        rg_all[r] = jnp.sum(jnp.where(spot, own_row, 0.0), axis=0, keepdims=True)
        share(rg_all, r, 14, col_peer, 32)
        own_col = jnp.sum(jnp.where(spot, own_cols, 0.0), axis=1, keepdims=True)
        cg_all[c] = jnp.where(my_lane, own_col, 0.0)
        share(cg_all, c, 15, row_peer, 8)

    with jax.named_scope("wait_grad"):
        arrived(s_all, 5, 8)
        arrived(g_recv, 6, 8)
        arrived(a_all, 2, 8)
    with jax.named_scope("wgrad"):
        s_sum = jnp.sum(s_all[...], axis=0)
        my_cols = pl.ds(pl.multiple_of(c * 128, 128), 128)
        f_cols = u_all[:, :, my_cols].astype(F32).reshape(64, 128)
        g_sum = jnp.sum(g_recv[...].astype(F32), axis=0)
        emb_grad = (g_sum - f_cols * unpack_rows(s_sum)).astype(BF16)
        w_send[...] = dot(rows_of(a_all), emb_grad, TN).astype(BF16).reshape(32, 32, 128)
        w_recv[r] = w_send[r]
        scatter(w_send, w_recv, r, 8, col_peer, 32)
        l_all[r] = (
            jnp.sum(jnp.where(iota((8, 128), 1) == 8, s_sum, 0.0), axis=0, keepdims=True) * 0.125
        )
        share(l_all, r, 9, col_peer, 32)

    with jax.named_scope("wait_bulk"):
        arrived(u_col, 13, 32)
        arrived(t_row, 12, 8)
        arrived(rg_all, 14, 32)
        arrived(cg_all, 15, 8)
    with jax.named_scope("text"):
        every = rows_of(u_col)
        expo_t = jnp.exp(INV_TEMP * dot(rows_of(t_row), every, NT))
        rowsum_t = jnp.sum(rg_all[...], axis=0)
        colsum_t = unpack_rows(jnp.sum(cg_all[...], axis=0))
        probs_t = (expo_t * (0.5 / colsum_t + 0.5 / rowsum_t)).astype(BF16)
        h_send[...] = (INV_TEMP * dot(probs_t, every)).reshape(8, 8, 1024)
        h_recv[c] = h_send[c]
        scatter(h_send, h_recv, c, 7, row_peer, 8)

    with jax.named_scope("wait_w"):
        arrived(w_recv, 8, 32)

    def chunk(a1, b1, core1):
        y1, x1 = place(a1, b1)
        return wgrad.at[
            pl.ds(pl.multiple_of(y1 * 256, 256), 256),
            pl.ds(pl.multiple_of((x1 * 2 + core1) * 128, 128), 128),
        ]

    with jax.named_scope("first"):
        mine = wgrad.at[pl.ds(pl.multiple_of(r * 32, 32), 32), my_cols]
        mine[...] = jnp.sum(w_recv[...].astype(F32), axis=0).astype(BF16)

        def first(k, carry):
            pltpu.make_async_remote_copy(
                src_ref=mine, dst_ref=mine, send_sem=send.at[10], recv_sem=c1.at[a],
                device_id=plane_peer(k)[1], device_id_type=MESH,
            ).start()
            return carry

        lax.fori_loop(1, 32, first, 0)

    partner = (idx + 1 - 2 * core,)

    def forward(piece):
        pltpu.make_async_remote_copy(
            src_ref=piece, dst_ref=piece, send_sem=send.at[11], recv_sem=recv.at[10],
            device_id=partner, device_id_type=MESH,
        ).start()

    def second(j, carry):
        a1 = (a + j) % 4
        piece = chunk(a1, b, core)

        @pl.when(j == 0)
        def _():
            short = wgrad.at[pl.ds(0, 224), pl.ds(0, 128)]
            local(short, short, c1.at[a]).wait()

        @pl.when(j > 0)
        def _():
            local(piece, piece, c1.at[a1]).wait()

        for m in range(1, 4):
            pltpu.make_async_remote_copy(
                src_ref=piece, dst_ref=piece, send_sem=send.at[11],
                recv_sem=c2.at[b * 4 + a1],
                device_id=device(a, (b + m) % 4, z, core), device_id_type=MESH,
            ).start()
        forward(piece)
        return carry

    with jax.named_scope("second"):
        lax.fori_loop(0, 4, second, 0)

    def third(t, carry):
        a1 = (a + t // 3) % 4
        b1 = (b + 1 + t % 3) % 4
        piece = chunk(a1, b1, core)
        local(piece, piece, c2.at[b1 * 4 + a1]).wait()
        forward(piece)
        return carry

    with jax.named_scope("third"):
        lax.fori_loop(0, 12, third, 0)

    with jax.named_scope("text_out"):
        arrived(h_recv, 7, 8)
        g_txt = jnp.sum(h_recv[...], axis=0) - INV_TEMP * img_u.astype(F32)
        tgrad_ref[...] = (
            g_txt - txt_f * jnp.sum(txt_f * g_txt, axis=1, keepdims=True)
        ) / txt_norm
        arrived(l_all, 9, 32)
        total = jnp.sum(jnp.sum(l_all[...], axis=0), axis=1, keepdims=True)
        loss_ref[...] = jnp.broadcast_to(total * (1.0 / 4096.0), (1, 128))

    with jax.named_scope("drain"):
        half = wgrad.at[:, pl.ds(0, 512)]
        local(half, half, recv.at[10]).wait()
        left(u_all, 0, 8)
        left(t_all, 1, 32)
        left(a_all, 2, 8)
        left(cs_all, 3, 32)
        left(rs_all, 4, 8)
        left(s_all, 5, 8)
        left(g_send, 6, 8)
        left(h_send, 7, 8)
        left(w_send, 8, 32)
        left(l_all, 9, 32)
        left(t_row, 12, 8)
        left(u_col, 13, 32)
        left(rg_all, 14, 32)
        left(cg_all, 15, 8)
        tall = wgrad.at[pl.ds(0, 992), pl.ds(0, 128)]
        local(tall, tall, send.at[10]).wait()
        wide = wgrad.at[:, pl.ds(0, 896)]
        local(wide, wide, send.at[11]).wait()


def step(features, gain, wq, wk, wv, wo, text):
    images, tokens, width = features.shape
    rows = images * tokens
    hbm = pl.BlockSpec(memory_space=pltpu.HBM)
    vmem = pl.BlockSpec(memory_space=pltpu.VMEM)
    return pl.pallas_call(
        step_kernel,
        out_shape=[
            jax.ShapeDtypeStruct((width, width), BF16),
            jax.ShapeDtypeStruct((images, width), F32),
            jax.ShapeDtypeStruct((1, 128), F32),
        ],
        in_specs=[hbm, vmem, hbm, hbm, hbm, hbm, vmem],
        out_specs=[vmem, vmem, vmem],
        scratch_shapes=[
            pltpu.VMEM((images, tokens, width), BF16),
            *[pltpu.VMEM((width, width), BF16)] * 4,
            *[pltpu.VMEM((rows, width), BF16)] * 4,
            pltpu.VMEM((images, width), F32),
            pltpu.VMEM((images, width), F32),
            pltpu.SemaphoreType.DMA((images,)),
            pltpu.SemaphoreType.DMA((4,)),
            pltpu.VMEM((32, 8, width), BF16),
            pltpu.VMEM((8, 8, width), BF16),
            pltpu.VMEM((8, 8, width), BF16),
            pltpu.VMEM((32, 8, width), BF16),
            pltpu.VMEM((8, 8, width), BF16),
            pltpu.VMEM((8, 8, 128), F32),
            pltpu.VMEM((32, 1, 256), F32),
            pltpu.VMEM((32, 1, 256), F32),
            pltpu.VMEM((8, 8, 128), F32),
            pltpu.VMEM((8, 64, 128), BF16),
            pltpu.VMEM((8, 64, 128), BF16),
            pltpu.VMEM((8, 8, 128), F32),
            pltpu.VMEM((8, 8, width), F32),
            pltpu.VMEM((8, 8, width), F32),
            pltpu.VMEM((32, 32, 128), BF16),
            pltpu.VMEM((32, 32, 128), BF16),
            pltpu.VMEM((32, 1, 128), F32),
            pltpu.SemaphoreType.DMA((16,)),
            pltpu.SemaphoreType.DMA((16,)),
            pltpu.SemaphoreType.DMA((4,)),
            pltpu.SemaphoreType.DMA((16,)),
        ],
        compiler_params=pltpu.CompilerParams(
            collective_id=0, has_side_effects=True, vmem_limit_bytes=64 * 1024 * 1000
        ),
        name="step",
    )(features, gain, wq, wk, wv, wo, text)


def whole(features, ln_gain, w_query, w_key, w_value, w_out, text_raw):
    wgrad, tgrad, loss = step(
        features, ln_gain.reshape(1, -1), w_query, w_key, w_value, w_out, text_raw
    )
    return (loss[0, 0], tgrad, wgrad)


def solution(mesh):
    placed = (P("dp", None, None), P(), P(), P(), P(), P(), P("dp", None))
    return jax.shard_map(
        whole, mesh=mesh, in_specs=placed, out_specs=(P(), P("dp", None), P()), check_vma=False
    )
```

time: 107 us -> 91.9 us (0.86)
  Pallas kernels: 99.1 us -> 84.9 us
  local copies, waits for them, and re-layouts: 5.8 us -> 4.45 us
    pallas_call x2 -> x1, Pallas kernels: 99.1 us -> 84.9 us  [step(): pl.pallas_call(step_kernel, out_shape=[jax.ShapeDtypeStruct((width, width...]
    unnamed x10 -> x2, local copies, waits for them, and re-layouts: 5.8 us -> 4.45 us
where the time goes in v2:
time: 91.9 us; the launch traced here: 91.7 us
  Pallas kernels  84.9 us (92%)
  local copies, waits for them, and re-layouts  4.45 us (5%)
  between operations  2.31 us (3%)
    pallas_call x1, Pallas kernels, step(): pl.pallas_call(step_kernel, out_shape=[jax.ShapeDtypeStruct((width, width...  84.9 us
    unnamed x2, local copies, waits for them, and re-layouts  4.45 us

profile of v2, /device:TPU:1, one launch (start us, length us, event | category | flops | bytes accessed | tf_op | source)
XLA Modules:
  0.0 91.7 jit_solution(10226013451488421230)
XLA Ops:
  0.6 84.9 %step.1 = (bf16[1024,1024]{1,0:T(8,128)(2,1)}, f32[8,1024]{1,0:T(8,128)}, f32[1,128]{1,0:T(1,128)}) custom-call(bf16[8,128,1024]{2,1,0:T(8,128)(2,1)} %feat_hbm.1, f32[1,1024]{1,0:T(1,128)} %bitcast.3, bf16[1024,1024]{1,0:T(8,128)(2,1)} %wq_hbm.1, bf16[1024,1024]{1,0:T(8,128)(2,1)} %wk_hbm.1, bf16[1024,1024]{1,0:T(8,128)(2,1)} %wv_hbm.1, ...), custom_call_target="tpu_custom_call" | custom-call | tf_op jit(solution)/shard_map/step/pallas_call | solution.py:430
  86.1 1.4 %copy.14 = f32[8,1024]{1,0:T(8,128)} copy(f32[8,1024]{1,0:T(8,128)} %get-tuple-element.13) | data formatting | bytes 65536
  87.5 3.1 %copy.15 = bf16[1024,1024]{1,0:T(8,128)(2,1)} copy(bf16[1024,1024]{1,0:T(8,128)(2,1)} %get-tuple-element.14) | data formatting | bytes 4194304

commit v3 on v2

--- a/solution.py
+++ b/solution.py
@@ -42,27 +42,37 @@
 
 
 def step_kernel(
-    feat_hbm, gain_ref, wq_hbm, wk_hbm, wv_hbm, wo_hbm, text_ref,
+    feat_hbm, gain_hbm, wq_hbm, wk_hbm, wv_hbm, wo_hbm, text_hbm,
     wgrad, tgrad_ref, loss_ref,
-    feat, wq, wk, wv, wo, normed, qh, kh, vh, abar_f, xbar, fsem, wsem,
+    feat, wq, wk, wv, wo, normed, qh, kh, vh, abar_f, xbar, gain_v, text_v, fsem, wsem,
     t_all, t_row, u_all, u_col, a_all, rs_all, cs_all, rg_all, cg_all,
     g_send, g_recv, s_all, h_send, h_recv, w_send, w_recv, l_all, send, recv, c1, c2,
 ):
+    div, rem = lax.div, lax.rem
     idx = lax.axis_index("dp")
-    core = idx % 2
-    z = (idx // 2) % 8
-    x = (idx // 16) % 4
-    y = idx // 64
+    core = rem(idx, 2)
+    z = rem(div(idx, 2), 8)
+    x = rem(div(idx, 16), 4)
+    y = div(idx, 64)
     c = x * 2 + core
     r = y * 8 + z
+    q = div(idx, 16) * 2 + core
 
     def row_peer(k):
-        p = (c + k) % 8
-        return p, (y * 64 + (p // 2) * 16 + z * 2 + p % 2,)
+        p = rem(c + k, 8)
+        return p, (y * 64 + div(p, 2) * 16 + z * 2 + rem(p, 2),)
 
     def col_peer(k):
-        p = (r + k) % 32
-        return p, ((p // 8) * 64 + x * 16 + (p % 8) * 2 + core,)
+        p = rem(r + k, 32)
+        return p, (div(p, 8) * 64 + x * 16 + rem(p, 8) * 2 + core,)
+
+    def ring_peer(k):
+        p = rem(z + k, 8)
+        return p, (idx + (p - z) * 2,)
+
+    def side_peer(k):
+        p = rem(q + k, 32)
+        return p, (div(p, 2) * 16 + z * 2 + rem(p, 2),)
 
     a = y * (1 - core) + x * core
     b = x * (1 - core) + y * core
@@ -77,8 +87,13 @@
         return (y1 * 64 + x1 * 16 + z1 * 2 + core1,)
 
     def plane_peer(k):
-        p = (a * 8 + z + k) % 32
-        return p, device(p // 8, b, p % 8, core)
+        p = rem(a * 8 + z + k, 32)
+        return p, device(div(p, 8), b, rem(p, 8), core)
+
+    def b_peer(k):
+        return rem(b + k, 4), device(a, rem(b + k, 4), z, core)
+
+    partner = (idx + 1 - 2 * core,)
 
     images = feat.shape[0]
     fcopy = [
@@ -86,7 +101,9 @@
     ]
     pairs = ((wq_hbm, wq), (wk_hbm, wk), (wv_hbm, wv), (wo_hbm, wo))
     wcopy = [pltpu.make_async_copy(s, d, wsem.at[i]) for i, (s, d) in enumerate(pairs)]
-    for cp in fcopy + wcopy:
+    gcopy = pltpu.make_async_copy(gain_hbm, gain_v, wsem.at[4])
+    tcopy = pltpu.make_async_copy(text_hbm, text_v, wsem.at[5])
+    for cp in [gcopy, *fcopy, *wcopy, tcopy]:
         cp.start()
 
     barrier = pltpu.get_barrier_semaphore()
@@ -98,9 +115,9 @@
 
         return step
 
-    lax.fori_loop(1, 8, greet(row_peer), 0)
-    lax.fori_loop(1, 32, greet(col_peer), 0)
-    lax.fori_loop(1, 32, greet(plane_peer), 0)
+    lax.fori_loop(1, 32, greet(col_peer), 0, unroll=True)
+    lax.fori_loop(1, 32, greet(side_peer), 0, unroll=True)
+    lax.fori_loop(1, 32, greet(plane_peer), 0, unroll=True)
 
     def push(src, dst, s, dev):
         pltpu.make_async_remote_copy(
@@ -113,7 +130,7 @@
             push(buf.at[slot], buf.at[slot], s, peer(k)[1])
             return carry
 
-        lax.fori_loop(1, n, step, 0)
+        lax.fori_loop(1, n, step, 0, unroll=True)
 
     def scatter(src, dst, slot, s, peer, n):
         def step(k, carry):
@@ -121,7 +138,7 @@
             push(src.at[p], dst.at[slot], s, dev)
             return carry
 
-        lax.fori_loop(1, n, step, 0)
+        lax.fori_loop(1, n, step, 0, unroll=True)
 
     def local(src, dst, sem):
         return pltpu.make_async_copy(src, dst, sem)
@@ -134,63 +151,60 @@
         part = buf.at[pl.ds(0, n - 1)]
         local(part, part, send.at[s]).wait()
 
-    text = text_ref[...].astype(F32)
-    txt_norm = jnp.sqrt(jnp.sum(text * text, axis=1, keepdims=True) + EPS)
-    txt_f = text / txt_norm
-    txt_u = txt_f.astype(BF16)
-    t_all[r] = txt_u
-    t_row[c] = txt_u
-    gain = gain_ref[...]
+    gcopy.wait()
+    gain = gain_v[...]
 
     with jax.named_scope("norm"):
         for i in range(images):
             fcopy[i].wait()
 
-            def norm_rows(t, total, i=i):
-                rows = pl.ds(pl.multiple_of(t * 32, 32), 32)
-                x = feat[i, rows, :].astype(F32)
-                center = x - jnp.mean(x, axis=-1, keepdims=True)
+            total = jnp.zeros((8, 1024), F32)
+            for t in range(2):
+                rows = slice(t * 64, t * 64 + 64)
+                tok = feat[i, rows, :].astype(F32)
+                center = tok - jnp.mean(tok, axis=-1, keepdims=True)
                 spread = jnp.mean(center * center, axis=-1, keepdims=True)
                 out = center * lax.rsqrt(spread + EPS) * gain
-                normed[pl.ds(pl.multiple_of(i * 128 + t * 32, 32), 32), :] = out.astype(BF16)
-                return total + jnp.sum(x.reshape(4, 8, 1024), axis=0)
-
-            total = lax.fori_loop(0, 4, norm_rows, jnp.zeros((8, 1024), F32))
+                normed[i * 128 + t * 64 : i * 128 + t * 64 + 64, :] = out.astype(BF16)
+                total = total + jnp.sum(tok.reshape(8, 8, 1024), axis=0)
             total = jnp.sum(total, axis=0, keepdims=True)
             first = feat[i, 0:16, :].astype(F32)[0:1]
             xbar[i : i + 1, :] = first + (total - first) * (1.0 / 127.0)
 
-    with jax.named_scope("greet"):
-        pl.semaphore_wait(barrier, 7 + 31 + 31)
-        share(t_all, r, 1, col_peer, 32)
-        share(t_row, c, 12, row_peer, 8)
-
     same_head = jnp.where(
         iota((256, 256), 0) // 64 == iota((256, 256), 1) // 64, 1.0, 0.0
     ).astype(BF16)
 
-    def project(w, out, scale):
-        def step(t, carry):
-            rows = pl.ds(pl.multiple_of((t % 2) * 512, 512), 512)
-            cols = pl.ds(pl.multiple_of((t // 2) * 256, 256), 256)
-            proj = dot(normed[rows, :], w[:, cols])
-            if scale is not None:
-                squares = dot((proj * proj).astype(BF16), same_head)
-                proj = proj * (lax.rsqrt(squares + EPS) * scale)
-            out[rows, cols] = proj.astype(BF16)
-            return carry
-
-        lax.fori_loop(0, 8, step, 0)
-
-    with jax.named_scope("query"):
-        wcopy[0].wait()
-        project(wq, qh, 8.0 * LOG2E)
-    with jax.named_scope("key"):
-        wcopy[1].wait()
-        project(wk, kh, 1.0)
-    with jax.named_scope("value"):
-        wcopy[2].wait()
-        project(wv, vh, None)
+    def unit(proj, scale):
+        squares = dot((proj * proj).astype(BF16), same_head)
+        return (proj * (lax.rsqrt(squares + EPS) * scale)).astype(BF16)
+
+    def project(t, carry):
+        cols = pl.ds(pl.multiple_of(t * 256, 256), 256)
+        tokens = normed[...]
+        query = dot(tokens, wq[:, cols])
+        key = dot(tokens, wk[:, cols])
+        qh[:, cols] = unit(query, 8.0 * LOG2E)
+        kh[:, cols] = unit(key, 1.0)
+        vh[:, cols] = dot(tokens, wv[:, cols]).astype(BF16)
+        return carry
+
+    with jax.named_scope("greet"):
+        tcopy.wait()
+        text = text_v[...].astype(F32)
+        txt_norm = jnp.sqrt(jnp.sum(text * text, axis=1, keepdims=True) + EPS)
+        txt_f = text / txt_norm
+        txt_u = txt_f.astype(BF16)
+        t_all[r] = txt_u
+        t_row[z] = txt_u
+        pl.semaphore_wait(barrier, 31 + 31 + 31)
+        share(t_all, r, 1, col_peer, 32)
+        share(t_row, z, 12, ring_peer, 8)
+
+    with jax.named_scope("project"):
+        for i in range(3):
+            wcopy[i].wait()
+        lax.fori_loop(0, 4, project, 0)
 
     lane = iota((1, 128), 1)
     low = jnp.where(lane < 64, 1.0, 0.0).astype(BF16)
@@ -209,9 +223,15 @@
             both = jnp.concatenate([q * low, q * high], axis=0)
             expo = jnp.exp2(dot(kh[rows, cols], both, NT))
             weight = weigh / jnp.sum(expo, axis=0, keepdims=True)
-            pooled = dot((expo * weight).astype(BF16), gather)
-            parts.append(jnp.sum(pooled * vh[rows, cols].astype(F32), axis=0, keepdims=True))
-        abar_f[pl.ds(i, 1), :] = jnp.concatenate(parts, axis=1)
+            parts.append((expo * weight).astype(BF16))
+        pooled = dot(jnp.concatenate(parts, axis=0), gather)
+        sums = []
+        for p in range(8):
+            value = vh[rows, p * 128 : p * 128 + 128].astype(F32)
+            sums.append(
+                jnp.sum(pooled[p * 128 : p * 128 + 128] * value, axis=0, keepdims=True)
+            )
+        abar_f[pl.ds(i, 1), :] = jnp.concatenate(sums, axis=1)
         return carry
 
     with jax.named_scope("attend"):
@@ -224,7 +244,7 @@
         emb_norm = jnp.sqrt(jnp.sum(emb * emb, axis=1, keepdims=True) + EPS)
         img_u = (emb / emb_norm).astype(BF16)
         u_all[c] = img_u
-        u_col[r] = img_u
+        u_col[q] = img_u
         a_all[c] = (abar.astype(F32) / emb_norm).astype(BF16)
         share(u_all, c, 0, row_peer, 8)
         share(a_all, c, 2, row_peer, 8)
@@ -246,7 +266,7 @@
         share(cs_all, r, 3, col_peer, 32)
         rs_all[c] = pack_rows(jnp.sum(expo, axis=1, keepdims=True))
         share(rs_all, c, 4, row_peer, 8)
-        share(u_col, r, 13, col_peer, 32)
+        share(u_col, q, 13, side_peer, 32)
     with jax.named_scope("wait_sums"):
         arrived(rs_all, 4, 8)
         arrived(cs_all, 3, 32)
@@ -282,12 +302,12 @@
         s_all[c] = jnp.where(iota((8, 128), 1) == 8, loss, pack_rows(s_part))
         share(s_all, c, 5, row_peer, 8)
         own_row = jnp.sum(own_rows, axis=1, keepdims=True)
-        spot = iota((8, 256), 1) - r * 8 == iota((8, 256), 0)
-        rg_all[r] = jnp.sum(jnp.where(spot, own_row, 0.0), axis=0, keepdims=True)
-        share(rg_all, r, 14, col_peer, 32)
-        own_col = jnp.sum(jnp.where(spot, own_cols, 0.0), axis=1, keepdims=True)
-        cg_all[c] = jnp.where(my_lane, own_col, 0.0)
-        share(cg_all, c, 15, row_peer, 8)
+        spot = iota((8, 256), 1) - iota((8, 256), 0)
+        rg_all[q] = jnp.sum(jnp.where(spot == q * 8, own_row, 0.0), axis=0, keepdims=True)
+        share(rg_all, q, 14, side_peer, 32)
+        own_col = jnp.sum(jnp.where(spot == r * 8, own_cols, 0.0), axis=1, keepdims=True)
+        cg_all[z] = jnp.where(iota((8, 128), 1) == z, own_col, 0.0)
+        share(cg_all, z, 15, ring_peer, 8)
 
     with jax.named_scope("wait_grad"):
         arrived(s_all, 5, 8)
@@ -318,80 +338,70 @@
         rowsum_t = jnp.sum(rg_all[...], axis=0)
         colsum_t = unpack_rows(jnp.sum(cg_all[...], axis=0))
         probs_t = (expo_t * (0.5 / colsum_t + 0.5 / rowsum_t)).astype(BF16)
-        h_send[...] = (INV_TEMP * dot(probs_t, every)).reshape(8, 8, 1024)
-        h_recv[c] = h_send[c]
-        scatter(h_send, h_recv, c, 7, row_peer, 8)
+        h_send[...] = (INV_TEMP * dot(probs_t, every)).reshape(8, 8, 1024).astype(BF16)
+        h_recv[z] = h_send[z]
 
     with jax.named_scope("wait_w"):
         arrived(w_recv, 8, 32)
 
-    def chunk(a1, b1, core1):
+    def part(a1, b1, first, size):
         y1, x1 = place(a1, b1)
         return wgrad.at[
-            pl.ds(pl.multiple_of(y1 * 256, 256), 256),
-            pl.ds(pl.multiple_of((x1 * 2 + core1) * 128, 128), 128),
+            pl.ds(pl.multiple_of(y1 * 256 + first, 32), size),
+            pl.ds(pl.multiple_of((x1 * 2 + core) * 128, 128), 128),
         ]
 
+    def block(a1, b1, z1):
+        return part(a1, b1, z1 * 32, 32)
+
+    def chunk(a1, b1):
+        return part(a1, b1, 0, 256)
+
+    def pass_on(piece, s, arrival, dev):
+        pltpu.make_async_remote_copy(
+            src_ref=piece, dst_ref=piece, send_sem=send.at[s], recv_sem=arrival,
+            device_id=dev, device_id_type=MESH,
+        ).start()
+
+    def to_b(piece, a1):
+        for m in (2, 1, 3):
+            pass_on(piece, 11, c2.at[b * 4 + a1], b_peer(m)[1])
+
+    order = sorted(
+        [(i, j) for i in range(4) for j in range(8) if i or j],
+        key=lambda t: (min(t[1], 8 - t[1]) + min(t[0], 4 - t[0]), t),
+    )
+
     with jax.named_scope("first"):
-        mine = wgrad.at[pl.ds(pl.multiple_of(r * 32, 32), 32), my_cols]
+        mine = block(a, b, z)
         mine[...] = jnp.sum(w_recv[...].astype(F32), axis=0).astype(BF16)
-
-        def first(k, carry):
-            pltpu.make_async_remote_copy(
-                src_ref=mine, dst_ref=mine, send_sem=send.at[10], recv_sem=c1.at[a],
-                device_id=plane_peer(k)[1], device_id_type=MESH,
-            ).start()
-            return carry
-
-        lax.fori_loop(1, 32, first, 0)
-
-    partner = (idx + 1 - 2 * core,)
-
-    def forward(piece):
-        pltpu.make_async_remote_copy(
-            src_ref=piece, dst_ref=piece, send_sem=send.at[11], recv_sem=recv.at[10],
-            device_id=partner, device_id_type=MESH,
-        ).start()
-
-    def second(j, carry):
-        a1 = (a + j) % 4
-        piece = chunk(a1, b, core)
-
-        @pl.when(j == 0)
-        def _():
-            short = wgrad.at[pl.ds(0, 224), pl.ds(0, 128)]
-            local(short, short, c1.at[a]).wait()
-
-        @pl.when(j > 0)
-        def _():
-            local(piece, piece, c1.at[a1]).wait()
-
-        for m in range(1, 4):
-            pltpu.make_async_remote_copy(
-                src_ref=piece, dst_ref=piece, send_sem=send.at[11],
-                recv_sem=c2.at[b * 4 + a1],
-                device_id=device(a, (b + m) % 4, z, core), device_id_type=MESH,
-            ).start()
-        forward(piece)
+        for i, j in order:
+            pass_on(mine, 10, c1.at[a * 8 + z], device(rem(a + i, 4), b, rem(z + j, 8), core))
+        to_b(mine, a)
+
+    with jax.named_scope("second"):
+        for i, j in order:
+            a1, z1 = rem(a + 4 - i, 4), rem(z + 8 - j, 8)
+            piece = block(a1, b, z1)
+            local(piece, piece, c1.at[a1 * 8 + z1]).wait()
+            to_b(piece, a1)
+        for k in range(4):
+            pass_on(chunk(rem(a + k, 4), b), 11, recv.at[10], partner)
+        scatter(h_send, h_recv, z, 7, ring_peer, 8)
+
+    def fourth(t, carry):
+        a1, b1 = rem(a + div(t, 3), 4), rem(b + 1 + rem(t, 3), 4)
+        piece = chunk(a1, b1)
+        local(piece, piece, c2.at[b1 * 4 + a1]).wait()
+        pass_on(piece, 11, recv.at[10], partner)
         return carry
 
-    with jax.named_scope("second"):
-        lax.fori_loop(0, 4, second, 0)
-
-    def third(t, carry):
-        a1 = (a + t // 3) % 4
-        b1 = (b + 1 + t % 3) % 4
-        piece = chunk(a1, b1, core)
-        local(piece, piece, c2.at[b1 * 4 + a1]).wait()
-        forward(piece)
-        return carry
-
-    with jax.named_scope("third"):
-        lax.fori_loop(0, 12, third, 0)
+    with jax.named_scope("fourth"):
+        lax.fori_loop(0, 12, fourth, 0)
 
     with jax.named_scope("text_out"):
         arrived(h_recv, 7, 8)
-        g_txt = jnp.sum(h_recv[...], axis=0) - INV_TEMP * img_u.astype(F32)
+        g_txt = jnp.sum(h_recv[...].astype(F32), axis=0) - INV_TEMP * img_u.astype(F32)
         tgrad_ref[...] = (
             g_txt - txt_f * jnp.sum(txt_f * g_txt, axis=1, keepdims=True)
         ) / txt_norm
@@ -400,7 +410,7 @@
         loss_ref[...] = jnp.broadcast_to(total * (1.0 / 4096.0), (1, 128))
 
     with jax.named_scope("drain"):
-        half = wgrad.at[:, pl.ds(0, 512)]
+        half = wgrad.at[pl.ds(0, 512)]
         local(half, half, recv.at[10]).wait()
         left(u_all, 0, 8)
         left(t_all, 1, 32)
@@ -418,7 +428,7 @@
         left(cg_all, 15, 8)
         tall = wgrad.at[pl.ds(0, 992), pl.ds(0, 128)]
         local(tall, tall, send.at[10]).wait()
-        wide = wgrad.at[:, pl.ds(0, 896)]
+        wide = wgrad.at[pl.ds(0, 896)]
         local(wide, wide, send.at[11]).wait()
 
 
@@ -434,7 +444,7 @@
             jax.ShapeDtypeStruct((images, width), F32),
             jax.ShapeDtypeStruct((1, 128), F32),
         ],
-        in_specs=[hbm, vmem, hbm, hbm, hbm, hbm, vmem],
+        in_specs=[hbm] * 7,
         out_specs=[vmem, vmem, vmem],
         scratch_shapes=[
             pltpu.VMEM((images, tokens, width), BF16),
@@ -442,8 +452,10 @@
             *[pltpu.VMEM((rows, width), BF16)] * 4,
             pltpu.VMEM((images, width), F32),
             pltpu.VMEM((images, width), F32),
+            pltpu.VMEM((1, width), F32),
+            pltpu.VMEM((images, width), BF16),
             pltpu.SemaphoreType.DMA((images,)),
-            pltpu.SemaphoreType.DMA((4,)),
+            pltpu.SemaphoreType.DMA((6,)),
             pltpu.VMEM((32, 8, width), BF16),
             pltpu.VMEM((8, 8, width), BF16),
             pltpu.VMEM((8, 8, width), BF16),
@@ -456,27 +468,26 @@
             pltpu.VMEM((8, 64, 128), BF16),
             pltpu.VMEM((8, 64, 128), BF16),
             pltpu.VMEM((8, 8, 128), F32),
-            pltpu.VMEM((8, 8, width), F32),
-            pltpu.VMEM((8, 8, width), F32),
+            pltpu.VMEM((8, 8, width), BF16),
+            pltpu.VMEM((8, 8, width), BF16),
             pltpu.VMEM((32, 32, 128), BF16),
             pltpu.VMEM((32, 32, 128), BF16),
             pltpu.VMEM((32, 1, 128), F32),
             pltpu.SemaphoreType.DMA((16,)),
             pltpu.SemaphoreType.DMA((16,)),
-            pltpu.SemaphoreType.DMA((4,)),
+            pltpu.SemaphoreType.DMA((32,)),
             pltpu.SemaphoreType.DMA((16,)),
         ],
         compiler_params=pltpu.CompilerParams(
-            collective_id=0, has_side_effects=True, vmem_limit_bytes=64 * 1024 * 1000
+            collective_id=0, has_side_effects=True, vmem_limit_bytes=40 << 20
         ),
         name="step",
     )(features, gain, wq, wk, wv, wo, text)
 
 
 def whole(features, ln_gain, w_query, w_key, w_value, w_out, text_raw):
-    wgrad, tgrad, loss = step(
-        features, ln_gain.reshape(1, -1), w_query, w_key, w_value, w_out, text_raw
-    )
+    args = (features, ln_gain.reshape(1, -1), w_query, w_key, w_value, w_out, text_raw)
+    wgrad, tgrad, loss = step(*(pltpu.with_memory_space_constraint(v, pltpu.HBM) for v in args))
     return (loss[0, 0], tgrad, wgrad)
 
 

time: 91.9 us -> 73 us (0.79)
  Pallas kernels: 84.9 us -> 69.2 us
  local copies, waits for them, and re-layouts: 4.45 us -> 1.94 us
    pallas_call x1, Pallas kernels: 84.9 us -> 69.2 us  [step(): pl.pallas_call(step_kernel, out_shape=[jax.ShapeDtypeStruct((width, width...]
    unnamed x2, local copies, waits for them, and re-layouts: 4.45 us -> 1.94 us
where the time goes in v3:
time: 73 us
  Pallas kernels  69.2 us (95%)
  local copies, waits for them, and re-layouts  1.94 us (3%)
  between operations  1.8 us (2%)
    pallas_call x1, Pallas kernels, step(): pl.pallas_call(step_kernel, out_shape=[jax.ShapeDtypeStruct((width, width...  69.2 us
    unnamed x2, local copies, waits for them, and re-layouts  1.94 us

profile of v3, /device:TPU:1, one launch (start us, length us, event | category | flops | bytes accessed | tf_op | source)
XLA Modules:
  0.0 73.0 jit_solution(5546786106821669749)
XLA Ops:
  0.6 69.2 %step.1 = (bf16[1024,1024]{1,0:T(8,128)(2,1)S(1)}, f32[8,1024]{1,0:T(8,128)S(1)}, f32[1,128]{1,0:T(1,128)S(1)}) custom-call(bf16[8,128,1024]{2,1,0:T(8,128)(2,1)} %feat_hbm.1, f32[1,1024]{1,0:T(1,128)} %bitcast.4, bf16[1024,1024]{1,0:T(8,128)(2,1)} %wq_hbm.1, bf16[1024,1024]{1,0:T(8,128)(2,1)} %wk_hbm.1, bf16[1024,1024]{1,0:T(8,128)(2,1)} %wv_hbm.1, ...), custom_call_target="tpu_custom_call" | custom-call | tf_op jit(solution)/shard_map/step/pallas_call | solution.py:440
  69.9 0.6 copy.14
  70.5 1.3 %copy.15 = bf16[1024,1024]{1,0:T(8,128)(2,1)} copy(bf16[1024,1024]{1,0:T(8,128)(2,1)S(1)} %get-tuple-element.14) | data formatting | bytes 4194304

commit v4 on v3

--- a/solution.py
+++ b/solution.py
@@ -58,21 +58,32 @@
     r = y * 8 + z
     q = div(idx, 16) * 2 + core
 
-    def row_peer(k):
-        p = rem(c + k, 8)
-        return p, (y * 64 + div(p, 2) * 16 + z * 2 + rem(p, 2),)
-
-    def col_peer(k):
-        p = rem(r + k, 32)
-        return p, (div(p, 8) * 64 + x * 16 + rem(p, 8) * 2 + core,)
-
-    def ring_peer(k):
-        p = rem(z + k, 8)
-        return p, (idx + (p - z) * 2,)
-
-    def side_peer(k):
-        p = rem(q + k, 32)
-        return p, (div(p, 2) * 16 + z * 2 + rem(p, 2),)
+    ys, xs = [[rem(v + i, 4) for i in range(4)] for v in (y, x)]
+    zs = [rem(z + j, 8) for j in range(8)]
+    other = 1 - core
+
+    def at(y1, x1, z1, core1):
+        return (y1 * 64 + x1 * 16 + z1 * 2 + core1,)
+
+    row_group = [
+        (xs[i] * 2 + n, at(y, xs[i], z, n))
+        for i in (2, 1, 3, 0)
+        for n in (other, core)
+        if i or n is other
+    ]
+    far = sorted(
+        [(i, j) for i in range(4) for j in range(8) if i or j],
+        key=lambda t: -min(t[0], 4 - t[0]) - min(t[1], 8 - t[1]),
+    )
+    col_group = [(ys[i] * 8 + zs[j], at(ys[i], x, zs[j], core)) for i, j in far]
+    ring_group = [(zs[j], at(y, x, zs[j], core)) for j in (4, 3, 5, 2, 6, 1, 7)]
+    side_group = [
+        (ys[i] * 8 + xs[k] * 2 + n, at(ys[i], xs[k], z, n))
+        for i in (2, 1, 3, 0)
+        for k in (2, 1, 3, 0)
+        for n in (other, core)
+        if i or k or n is other
+    ]
 
     a = y * (1 - core) + x * core
     b = x * (1 - core) + y * core
@@ -86,13 +97,7 @@
         y1, x1 = place(a1, b1)
         return (y1 * 64 + x1 * 16 + z1 * 2 + core1,)
 
-    def plane_peer(k):
-        p = rem(a * 8 + z + k, 32)
-        return p, device(div(p, 8), b, rem(p, 8), core)
-
-    def b_peer(k):
-        return rem(b + k, 4), device(a, rem(b + k, 4), z, core)
-
+    as_, bs = [[rem(v + i, 4) for i in range(4)] for v in (a, b)]
     partner = (idx + 1 - 2 * core,)
 
     images = feat.shape[0]
@@ -108,16 +113,13 @@
 
     barrier = pltpu.get_barrier_semaphore()
 
-    def greet(peer):
-        def step(k, carry):
-            pl.semaphore_signal(barrier, inc=1, device_id=peer(k)[1], device_id_type=MESH)
-            return carry
-
-        return step
-
-    lax.fori_loop(1, 32, greet(col_peer), 0, unroll=True)
-    lax.fori_loop(1, 32, greet(side_peer), 0, unroll=True)
-    lax.fori_loop(1, 32, greet(plane_peer), 0, unroll=True)
+    def greet(devices):
+        for dev in devices:
+            pl.semaphore_signal(barrier, inc=1, device_id=dev, device_id_type=MESH)
+
+    greet([dev for _, dev in col_group])
+    greet([dev for _, dev in side_group])
+    greet([device(as_[i], b, zs[j], core) for i, j in far])
 
     def push(src, dst, s, dev):
         pltpu.make_async_remote_copy(
@@ -125,20 +127,13 @@
             device_id=dev, device_id_type=MESH,
         ).start()
 
-    def share(buf, slot, s, peer, n):
-        def step(k, carry):
-            push(buf.at[slot], buf.at[slot], s, peer(k)[1])
-            return carry
-
-        lax.fori_loop(1, n, step, 0, unroll=True)
-
-    def scatter(src, dst, slot, s, peer, n):
-        def step(k, carry):
-            p, dev = peer(k)
+    def share(buf, slot, s, group):
+        for _, dev in group:
+            push(buf.at[slot], buf.at[slot], s, dev)
+
+    def scatter(src, dst, slot, s, group):
+        for p, dev in group:
             push(src.at[p], dst.at[slot], s, dev)
-            return carry
-
-        lax.fori_loop(1, n, step, 0, unroll=True)
 
     def local(src, dst, sem):
         return pltpu.make_async_copy(src, dst, sem)
@@ -189,6 +184,11 @@
         vh[:, cols] = dot(tokens, wv[:, cols]).astype(BF16)
         return carry
 
+    with jax.named_scope("project"):
+        for i in range(3):
+            wcopy[i].wait()
+        lax.fori_loop(0, 1, project, 0)
+
     with jax.named_scope("greet"):
         tcopy.wait()
         text = text_v[...].astype(F32)
@@ -198,13 +198,11 @@
         t_all[r] = txt_u
         t_row[z] = txt_u
         pl.semaphore_wait(barrier, 31 + 31 + 31)
-        share(t_all, r, 1, col_peer, 32)
-        share(t_row, z, 12, ring_peer, 8)
+        share(t_all, r, 1, col_group)
+        share(t_row, z, 12, ring_group)
 
     with jax.named_scope("project"):
-        for i in range(3):
-            wcopy[i].wait()
-        lax.fori_loop(0, 4, project, 0)
+        lax.fori_loop(1, 4, project, 0)
 
     lane = iota((1, 128), 1)
     low = jnp.where(lane < 64, 1.0, 0.0).astype(BF16)
@@ -216,21 +214,28 @@
 
     def attend(i, carry):
         rows = pl.ds(pl.multiple_of(i * 128, 128), 128)
-        parts = []
+        pooled = []
         for p in range(8):
             cols = slice(p * 128, p * 128 + 128)
             q = qh[rows, cols]
             both = jnp.concatenate([q * low, q * high], axis=0)
             expo = jnp.exp2(dot(kh[rows, cols], both, NT))
-            weight = weigh / jnp.sum(expo, axis=0, keepdims=True)
-            parts.append((expo * weight).astype(BF16))
-        pooled = dot(jnp.concatenate(parts, axis=0), gather)
-        sums = []
-        for p in range(8):
-            value = vh[rows, p * 128 : p * 128 + 128].astype(F32)
-            sums.append(
-                jnp.sum(pooled[p * 128 : p * 128 + 128] * value, axis=0, keepdims=True)
+            share_of = expo * (weigh / jnp.sum(expo, axis=0, keepdims=True))
+            if p < 4:
+                first = jnp.sum(share_of[:, :128], axis=1, keepdims=True)
+                second = jnp.sum(share_of[:, 128:], axis=1, keepdims=True)
+                pooled.append(jnp.where(lane < 64, first, second))
+            else:
+                pooled.append(share_of.astype(BF16))
+        if pooled[4:]:
+            rest = dot(jnp.concatenate(pooled[4:], axis=0), gather)
+            pooled[4:] = [rest[p * 128 : p * 128 + 128] for p in range(8 - 4)]
+        sums = [
+            jnp.sum(
+                pooled[p] * vh[rows, p * 128 : p * 128 + 128].astype(F32), axis=0, keepdims=True
             )
+            for p in range(8)
+        ]
         abar_f[pl.ds(i, 1), :] = jnp.concatenate(sums, axis=1)
         return carry
 
@@ -244,10 +249,9 @@
         emb_norm = jnp.sqrt(jnp.sum(emb * emb, axis=1, keepdims=True) + EPS)
         img_u = (emb / emb_norm).astype(BF16)
         u_all[c] = img_u
-        u_col[q] = img_u
         a_all[c] = (abar.astype(F32) / emb_norm).astype(BF16)
-        share(u_all, c, 0, row_peer, 8)
-        share(a_all, c, 2, row_peer, 8)
+        share(u_all, c, 0, row_group)
+        share(a_all, c, 2, row_group)
         diag = INV_TEMP * jnp.sum(
             jnp.sum(img_u.astype(F32) * txt_u.astype(F32), axis=1, keepdims=True),
             axis=0, keepdims=True,
@@ -263,10 +267,13 @@
         logits = INV_TEMP * dot(img, txt, NT)
         expo = jnp.exp(logits)
         cs_all[r] = jnp.sum(expo, axis=0, keepdims=True)
-        share(cs_all, r, 3, col_peer, 32)
+        share(cs_all, r, 3, col_group)
         rs_all[c] = pack_rows(jnp.sum(expo, axis=1, keepdims=True))
-        share(rs_all, c, 4, row_peer, 8)
-        share(u_col, q, 13, side_peer, 32)
+        share(rs_all, c, 4, row_group)
+        mine_y = pl.ds(y * 8, 8)
+        u_col[mine_y] = u_all[...]
+        for i in (2, 1, 3):
+            push(u_all, u_col.at[mine_y], 13, at(ys[i], x, z, core))
     with jax.named_scope("wait_sums"):
         arrived(rs_all, 4, 8)
         arrived(cs_all, 3, 32)
@@ -283,7 +290,7 @@
         for k in range(8):
             g_send[k] = grad[:, 128 * k : 128 * k + 128].astype(BF16)
         g_recv[c] = g_send[c]
-        scatter(g_send, g_recv, c, 6, row_peer, 8)
+        scatter(g_send, g_recv, c, 6, row_group)
         s_part = jnp.sum(delta.astype(F32) * logits, axis=1, keepdims=True)
         my_lane = iota((8, 128), 1) == c
         own_rows = jnp.where(my_lane, row_tile, 0.0)
@@ -300,14 +307,14 @@
             - 2.0 * diag
         )
         s_all[c] = jnp.where(iota((8, 128), 1) == 8, loss, pack_rows(s_part))
-        share(s_all, c, 5, row_peer, 8)
+        share(s_all, c, 5, row_group)
         own_row = jnp.sum(own_rows, axis=1, keepdims=True)
         spot = iota((8, 256), 1) - iota((8, 256), 0)
         rg_all[q] = jnp.sum(jnp.where(spot == q * 8, own_row, 0.0), axis=0, keepdims=True)
-        share(rg_all, q, 14, side_peer, 32)
+        share(rg_all, q, 14, side_group)
         own_col = jnp.sum(jnp.where(spot == r * 8, own_cols, 0.0), axis=1, keepdims=True)
         cg_all[z] = jnp.where(iota((8, 128), 1) == z, own_col, 0.0)
-        share(cg_all, z, 15, ring_peer, 8)
+        share(cg_all, z, 15, ring_group)
 
     with jax.named_scope("wait_grad"):
         arrived(s_all, 5, 8)
@@ -321,14 +328,14 @@
         emb_grad = (g_sum - f_cols * unpack_rows(s_sum)).astype(BF16)
         w_send[...] = dot(rows_of(a_all), emb_grad, TN).astype(BF16).reshape(32, 32, 128)
         w_recv[r] = w_send[r]
-        scatter(w_send, w_recv, r, 8, col_peer, 32)
+        scatter(w_send, w_recv, r, 8, col_group)
         l_all[r] = (
             jnp.sum(jnp.where(iota((8, 128), 1) == 8, s_sum, 0.0), axis=0, keepdims=True) * 0.125
         )
-        share(l_all, r, 9, col_peer, 32)
+        share(l_all, r, 9, col_group)
 
     with jax.named_scope("wait_bulk"):
-        arrived(u_col, 13, 32)
+        arrived(u_col, 13, 25)
         arrived(t_row, 12, 8)
         arrived(rg_all, 14, 32)
         arrived(cg_all, 15, 8)
@@ -365,29 +372,39 @@
 
     def to_b(piece, a1):
         for m in (2, 1, 3):
-            pass_on(piece, 11, c2.at[b * 4 + a1], b_peer(m)[1])
-
-    order = sorted(
-        [(i, j) for i in range(4) for j in range(8) if i or j],
-        key=lambda t: (min(t[1], 8 - t[1]) + min(t[0], 4 - t[0]), t),
-    )
+            pass_on(piece, 11, c2.at[b * 4 + a1], device(a, bs[m], z, core))
+
+    def to_a(piece, z1):
+        for m in (2, 1, 3):
+            pass_on(piece, 10, c1.at[a * 8 + z1], device(as_[m], b, z, core))
+
+    near = 4
+
+    def length(t):
+        i, j = min(t[0], 4 - t[0]), min(t[1], 8 - t[1])
+        return (i + j + (2.5 if i and j > near else 0.0), t)
+
+    order = sorted([(i, j) for i in range(4) for j in range(8) if i or j], key=length)
 
     with jax.named_scope("first"):
         mine = block(a, b, z)
         mine[...] = jnp.sum(w_recv[...].astype(F32), axis=0).astype(BF16)
         for i, j in order:
-            pass_on(mine, 10, c1.at[a * 8 + z], device(rem(a + i, 4), b, rem(z + j, 8), core))
+            if i == 0 or min(j, 8 - j) <= near:
+                pass_on(mine, 10, c1.at[a * 8 + z], device(as_[i], b, zs[j], core))
         to_b(mine, a)
 
     with jax.named_scope("second"):
         for i, j in order:
-            a1, z1 = rem(a + 4 - i, 4), rem(z + 8 - j, 8)
+            a1, z1 = as_[-i], zs[-j]
             piece = block(a1, b, z1)
             local(piece, piece, c1.at[a1 * 8 + z1]).wait()
+            if i == 0 and min(j, 8 - j) > near:
+                to_a(piece, z1)
             to_b(piece, a1)
         for k in range(4):
-            pass_on(chunk(rem(a + k, 4), b), 11, recv.at[10], partner)
-        scatter(h_send, h_recv, z, 7, ring_peer, 8)
+            pass_on(chunk(as_[k], b), 11, recv.at[10], partner)
+        scatter(h_send, h_recv, z, 7, ring_group)
 
     def fourth(t, carry):
         a1, b1 = rem(a + div(t, 3), 4), rem(b + 1 + rem(t, 3), 4)
@@ -423,7 +440,7 @@
         left(w_send, 8, 32)
         left(l_all, 9, 32)
         left(t_row, 12, 8)
-        left(u_col, 13, 32)
+        left(u_col, 13, 25)
         left(rg_all, 14, 32)
         left(cg_all, 15, 8)
         tall = wgrad.at[pl.ds(0, 992), pl.ds(0, 128)]

time: 73 us -> 68.9 us (0.944)
  Pallas kernels: 69.2 us -> 65 us
    pallas_call x1, Pallas kernels: 69.2 us -> 65 us  [step(): pl.pallas_call(step_kernel, out_shape=[jax.ShapeDtypeStruct((width, width...]
where the time goes in v4:
time: 68.9 us; the launch traced here: 68.8 us
  Pallas kernels  65 us (94%)
  local copies, waits for them, and re-layouts  1.94 us (3%)
  between operations  1.8 us (3%)
    pallas_call x1, Pallas kernels, step(): pl.pallas_call(step_kernel, out_shape=[jax.ShapeDtypeStruct((width, width...  65 us
    unnamed x2, local copies, waits for them, and re-layouts  1.94 us

profile of v4, /device:TPU:1, one launch (start us, length us, event | category | flops | bytes accessed | tf_op | source)
XLA Modules:
  0.0 68.8 jit_solution(3415249255984426321)
XLA Ops:
  0.6 65.0 %step.1 = (bf16[1024,1024]{1,0:T(8,128)(2,1)S(1)}, f32[8,1024]{1,0:T(8,128)S(1)}, f32[1,128]{1,0:T(1,128)S(1)}) custom-call(bf16[8,128,1024]{2,1,0:T(8,128)(2,1)} %feat_hbm.1, f32[1,1024]{1,0:T(1,128)} %bitcast.4, bf16[1024,1024]{1,0:T(8,128)(2,1)} %wq_hbm.1, bf16[1024,1024]{1,0:T(8,128)(2,1)} %wk_hbm.1, bf16[1024,1024]{1,0:T(8,128)(2,1)} %wv_hbm.1, ...), custom_call_target="tpu_custom_call" | custom-call | tf_op jit(solution)/shard_map/step/pallas_call | solution.py:457
  65.7 0.6 copy.14
  66.3 1.3 %copy.15 = bf16[1024,1024]{1,0:T(8,128)(2,1)} copy(bf16[1024,1024]{1,0:T(8,128)(2,1)S(1)} %get-tuple-element.14) | data formatting | bytes 4194304

commit v5 on v4

--- a/solution.py
+++ b/solution.py
@@ -326,9 +326,11 @@
         f_cols = u_all[:, :, my_cols].astype(F32).reshape(64, 128)
         g_sum = jnp.sum(g_recv[...].astype(F32), axis=0)
         emb_grad = (g_sum - f_cols * unpack_rows(s_sum)).astype(BF16)
-        w_send[...] = dot(rows_of(a_all), emb_grad, TN).astype(BF16).reshape(32, 32, 128)
-        w_recv[r] = w_send[r]
-        scatter(w_send, w_recv, r, 8, col_group)
+        partial = dot(rows_of(a_all), emb_grad, TN).reshape(32, 2, 16, 128)
+        for h in range(2):
+            w_send[h] = partial[:, h].astype(BF16)
+            w_recv[h, r] = w_send[h, r]
+            scatter(w_send.at[h], w_recv.at[h], r, (8, 16)[h], col_group)
         l_all[r] = (
             jnp.sum(jnp.where(iota((8, 128), 1) == 8, s_sum, 0.0), axis=0, keepdims=True) * 0.125
         )
@@ -348,18 +350,15 @@
         h_send[...] = (INV_TEMP * dot(probs_t, every)).reshape(8, 8, 1024).astype(BF16)
         h_recv[z] = h_send[z]
 
-    with jax.named_scope("wait_w"):
-        arrived(w_recv, 8, 32)
-
     def part(a1, b1, first, size):
         y1, x1 = place(a1, b1)
         return wgrad.at[
-            pl.ds(pl.multiple_of(y1 * 256 + first, 32), size),
+            pl.ds(pl.multiple_of(y1 * 256 + first, 16), size),
             pl.ds(pl.multiple_of((x1 * 2 + core) * 128, 128), 128),
         ]
 
-    def block(a1, b1, z1):
-        return part(a1, b1, z1 * 32, 32)
+    def block(a1, b1, z1, h):
+        return part(a1, b1, z1 * 32 + h * 16, 16)
 
     def chunk(a1, b1):
         return part(a1, b1, 0, 256)
@@ -374,33 +373,30 @@
         for m in (2, 1, 3):
             pass_on(piece, 11, c2.at[b * 4 + a1], device(a, bs[m], z, core))
 
-    def to_a(piece, z1):
-        for m in (2, 1, 3):
-            pass_on(piece, 10, c1.at[a * 8 + z1], device(as_[m], b, z, core))
-
-    near = 4
-
     def length(t):
         i, j = min(t[0], 4 - t[0]), min(t[1], 8 - t[1])
-        return (i + j + (2.5 if i and j > near else 0.0), t)
+        return (i + j, t)
 
     order = sorted([(i, j) for i in range(4) for j in range(8) if i or j], key=length)
 
-    with jax.named_scope("first"):
-        mine = block(a, b, z)
-        mine[...] = jnp.sum(w_recv[...].astype(F32), axis=0).astype(BF16)
-        for i, j in order:
-            if i == 0 or min(j, 8 - j) <= near:
-                pass_on(mine, 10, c1.at[a * 8 + z], device(as_[i], b, zs[j], core))
-        to_b(mine, a)
+    for h in range(2):
+        with jax.named_scope("wait_w"):
+            arrived(w_recv.at[h], (8, 16)[h], 32)
+        with jax.named_scope("first"):
+            mine = block(a, b, z, h)
+            mine[...] = jnp.sum(w_recv[h].astype(F32), axis=0).astype(BF16)
+            for i, j in order:
+                pass_on(mine, 10, c1.at[h, a * 8 + z], device(as_[i], b, zs[j], core))
+            to_b(mine, a)
 
     with jax.named_scope("second"):
-        for i, j in order:
+        for i, j, h in sorted(
+            [(i, j, h) for i, j in order for h in range(2)],
+            key=lambda t: (length(t[:2])[0] + 3.0 * t[2], t[2], t),
+        ):
             a1, z1 = as_[-i], zs[-j]
-            piece = block(a1, b, z1)
-            local(piece, piece, c1.at[a1 * 8 + z1]).wait()
-            if i == 0 and min(j, 8 - j) > near:
-                to_a(piece, z1)
+            piece = block(a1, b, z1, h)
+            local(piece, piece, c1.at[h, a1 * 8 + z1]).wait()
             to_b(piece, a1)
         for k in range(4):
             pass_on(chunk(as_[k], b), 11, recv.at[10], partner)
@@ -437,7 +433,8 @@
         left(s_all, 5, 8)
         left(g_send, 6, 8)
         left(h_send, 7, 8)
-        left(w_send, 8, 32)
+        left(w_send.at[0], 8, 32)
+        left(w_send.at[1], 16, 32)
         left(l_all, 9, 32)
         left(t_row, 12, 8)
         left(u_col, 13, 25)
@@ -487,12 +484,12 @@
             pltpu.VMEM((8, 8, 128), F32),
             pltpu.VMEM((8, 8, width), BF16),
             pltpu.VMEM((8, 8, width), BF16),
-            pltpu.VMEM((32, 32, 128), BF16),
-            pltpu.VMEM((32, 32, 128), BF16),
+            pltpu.VMEM((2, 32, 16, 128), BF16),
+            pltpu.VMEM((2, 32, 16, 128), BF16),
             pltpu.VMEM((32, 1, 128), F32),
-            pltpu.SemaphoreType.DMA((16,)),
-            pltpu.SemaphoreType.DMA((16,)),
-            pltpu.SemaphoreType.DMA((32,)),
+            pltpu.SemaphoreType.DMA((17,)),
+            pltpu.SemaphoreType.DMA((17,)),
+            pltpu.SemaphoreType.DMA((2, 32)),
             pltpu.SemaphoreType.DMA((16,)),
         ],
         compiler_params=pltpu.CompilerParams(
@@ -502,9 +499,34 @@
     )(features, gain, wq, wk, wv, wo, text)
 
 
+def finish_kernel(w_ref, t_ref, w_out, t_out, sems):
+    half = [pl.ds(512 * i, 512) for i in range(2)]
+    copies = [pltpu.make_async_copy(w_ref.at[h], w_out.at[h], sems.at[i]) for i, h in enumerate(half)]
+    copies.append(pltpu.make_async_copy(t_ref, t_out, sems.at[2]))
+    for cp in copies:
+        cp.start()
+    for cp in copies:
+        cp.wait()
+
+
+def finish(wgrad, tgrad):
+    any_spec = pl.BlockSpec(memory_space=pl.ANY)
+    hbm = pl.BlockSpec(memory_space=pltpu.HBM)
+    return pl.pallas_call(
+        finish_kernel,
+        out_shape=[jax.ShapeDtypeStruct(v.shape, v.dtype) for v in (wgrad, tgrad)],
+        in_specs=[any_spec, any_spec],
+        out_specs=[hbm, hbm],
+        scratch_shapes=[pltpu.SemaphoreType.DMA((3,))],
+        compiler_params=pltpu.CompilerParams(vmem_limit_bytes=1 << 20),
+        name="finish",
+    )(wgrad, tgrad)
+
+
 def whole(features, ln_gain, w_query, w_key, w_value, w_out, text_raw):
     args = (features, ln_gain.reshape(1, -1), w_query, w_key, w_value, w_out, text_raw)
     wgrad, tgrad, loss = step(*(pltpu.with_memory_space_constraint(v, pltpu.HBM) for v in args))
+    wgrad, tgrad = finish(wgrad, tgrad)
     return (loss[0, 0], tgrad, wgrad)
 
 

time: 68.9 us -> 68.1 us (0.988)
  local copies, waits for them, and re-layouts: 1.94 us -> 0 us
  Pallas kernels: 65 us -> 66.2 us
    unnamed x2 -> x0, local copies, waits for them, and re-layouts: 1.94 us -> none
    pallas_call x0 -> x1, Pallas kernels: none -> 1.35 us  [finish(): pl.pallas_call(finish_kernel, out_shape=[jax.ShapeDtypeStruct(v.shape, v....]
where the time goes in v5:
time: 68.1 us; the launch traced here: 68 us
  Pallas kernels  66.2 us (97%)
  between operations  1.81 us (3%)
    pallas_call x1, Pallas kernels, step(): pl.pallas_call(step_kernel, out_shape=[jax.ShapeDtypeStruct((width, width...  64.9 us

profile of v5, /device:TPU:1, one launch (start us, length us, event | category | flops | bytes accessed | tf_op | source)
XLA Modules:
  0.0 68.0 jit_solution(7690896194818099887)
XLA Ops:
  0.6 64.9 %step.1 = (bf16[1024,1024]{1,0:T(8,128)(2,1)S(1)}, f32[8,1024]{1,0:T(8,128)S(1)}, f32[1,128]{1,0:T(1,128)S(1)}) custom-call(bf16[8,128,1024]{2,1,0:T(8,128)(2,1)} %feat_hbm.1, f32[1,1024]{1,0:T(1,128)} %bitcast.4, bf16[1024,1024]{1,0:T(8,128)(2,1)} %wq_hbm.1, bf16[1024,1024]{1,0:T(8,128)(2,1)} %wk_hbm.1, bf16[1024,1024]{1,0:T(8,128)(2,1)} %wv_hbm.1, ...), custom_call_target="tpu_custom_call" | custom-call | tf_op jit(solution)/shard_map/step/pallas_call | solution.py:454
  65.5 1.3 %finish.1 = (bf16[1024,1024]{1,0:T(8,128)(2,1)}, f32[8,1024]{1,0:T(8,128)}) custom-call(bf16[1024,1024]{1,0:T(8,128)(2,1)S(1)} %get-tuple-element.9.w_ref, f32[8,1024]{1,0:T(8,128)S(1)} %get-tuple-element.10.t_ref), custom_call_target="tpu_custom_call" | custom-call | tf_op jit(solution)/shard_map/finish/pallas_call | solution.py:515

commit v6 on v5

--- a/solution.py
+++ b/solution.py
@@ -45,7 +45,7 @@
     feat_hbm, gain_hbm, wq_hbm, wk_hbm, wv_hbm, wo_hbm, text_hbm,
     wgrad, tgrad_ref, loss_ref,
     feat, wq, wk, wv, wo, normed, qh, kh, vh, abar_f, xbar, gain_v, text_v, fsem, wsem,
-    t_all, t_row, u_all, u_col, a_all, rs_all, cs_all, rg_all, cg_all,
+    txt_v, scaled_t, t_all, t_row, u_all, u_col, a_all, rs_all, cs_all, rg_all, cg_all,
     g_send, g_recv, s_all, h_send, h_recv, w_send, w_recv, l_all, send, recv, c1, c2,
 ):
     div, rem = lax.div, lax.rem
@@ -259,21 +259,18 @@
 
     with jax.named_scope("wait_text"):
         arrived(t_all, 1, 32)
+        txt_v[...] = rows_of(t_all)
     with jax.named_scope("wait_img"):
         arrived(u_all, 0, 8)
     with jax.named_scope("logits"):
         img = rows_of(u_all)
-        txt = rows_of(t_all)
+        txt = txt_v[...]
         logits = INV_TEMP * dot(img, txt, NT)
         expo = jnp.exp(logits)
         cs_all[r] = jnp.sum(expo, axis=0, keepdims=True)
         share(cs_all, r, 3, col_group)
         rs_all[c] = pack_rows(jnp.sum(expo, axis=1, keepdims=True))
         share(rs_all, c, 4, row_group)
-        mine_y = pl.ds(y * 8, 8)
-        u_col[mine_y] = u_all[...]
-        for i in (2, 1, 3):
-            push(u_all, u_col.at[mine_y], 13, at(ys[i], x, z, core))
     with jax.named_scope("wait_sums"):
         arrived(rs_all, 4, 8)
         arrived(cs_all, 3, 32)
@@ -315,18 +312,23 @@
         own_col = jnp.sum(jnp.where(spot == r * 8, own_cols, 0.0), axis=1, keepdims=True)
         cg_all[z] = jnp.where(iota((8, 128), 1) == z, own_col, 0.0)
         share(cg_all, z, 15, ring_group)
+        mine_y = pl.ds(y * 8, 8)
+        u_col[mine_y] = u_all[...]
+        for i in (2, 1, 3):
+            push(u_all, u_col.at[mine_y], 13, at(ys[i], x, z, core))
 
     with jax.named_scope("wait_grad"):
+        arrived(a_all, 2, 8)
+        scaled_t[...] = rows_of(a_all).T
         arrived(s_all, 5, 8)
         arrived(g_recv, 6, 8)
-        arrived(a_all, 2, 8)
     with jax.named_scope("wgrad"):
         s_sum = jnp.sum(s_all[...], axis=0)
         my_cols = pl.ds(pl.multiple_of(c * 128, 128), 128)
         f_cols = u_all[:, :, my_cols].astype(F32).reshape(64, 128)
         g_sum = jnp.sum(g_recv[...].astype(F32), axis=0)
         emb_grad = (g_sum - f_cols * unpack_rows(s_sum)).astype(BF16)
-        partial = dot(rows_of(a_all), emb_grad, TN).reshape(32, 2, 16, 128)
+        partial = dot(scaled_t[...], emb_grad).reshape(32, 2, 16, 128)
         for h in range(2):
             w_send[h] = partial[:, h].astype(BF16)
             w_recv[h, r] = w_send[h, r]
@@ -334,21 +336,6 @@
         l_all[r] = (
             jnp.sum(jnp.where(iota((8, 128), 1) == 8, s_sum, 0.0), axis=0, keepdims=True) * 0.125
         )
-        share(l_all, r, 9, col_group)
-
-    with jax.named_scope("wait_bulk"):
-        arrived(u_col, 13, 25)
-        arrived(t_row, 12, 8)
-        arrived(rg_all, 14, 32)
-        arrived(cg_all, 15, 8)
-    with jax.named_scope("text"):
-        every = rows_of(u_col)
-        expo_t = jnp.exp(INV_TEMP * dot(rows_of(t_row), every, NT))
-        rowsum_t = jnp.sum(rg_all[...], axis=0)
-        colsum_t = unpack_rows(jnp.sum(cg_all[...], axis=0))
-        probs_t = (expo_t * (0.5 / colsum_t + 0.5 / rowsum_t)).astype(BF16)
-        h_send[...] = (INV_TEMP * dot(probs_t, every)).reshape(8, 8, 1024).astype(BF16)
-        h_recv[z] = h_send[z]
 
     def part(a1, b1, first, size):
         y1, x1 = place(a1, b1)
@@ -388,8 +375,23 @@
             for i, j in order:
                 pass_on(mine, 10, c1.at[h, a * 8 + z], device(as_[i], b, zs[j], core))
             to_b(mine, a)
+        if h == 0:
+            with jax.named_scope("wait_bulk"):
+                arrived(u_col, 13, 25)
+                arrived(t_row, 12, 8)
+                arrived(rg_all, 14, 32)
+                arrived(cg_all, 15, 8)
+            with jax.named_scope("text"):
+                every = rows_of(u_col)
+                expo_t = jnp.exp(INV_TEMP * dot(rows_of(t_row), every, NT))
+                rowsum_t = jnp.sum(rg_all[...], axis=0)
+                colsum_t = unpack_rows(jnp.sum(cg_all[...], axis=0))
+                probs_t = (expo_t * (0.5 / colsum_t + 0.5 / rowsum_t)).astype(BF16)
+                h_send[...] = (INV_TEMP * dot(probs_t, every)).reshape(8, 8, 1024).astype(BF16)
+                h_recv[z] = h_send[z]
 
     with jax.named_scope("second"):
+        share(l_all, r, 9, col_group)
         for i, j, h in sorted(
             [(i, j, h) for i, j in order for h in range(2)],
             key=lambda t: (length(t[:2])[0] + 3.0 * t[2], t[2], t),
@@ -470,6 +472,8 @@
             pltpu.VMEM((images, width), BF16),
             pltpu.SemaphoreType.DMA((images,)),
             pltpu.SemaphoreType.DMA((6,)),
+            pltpu.VMEM((256, width), BF16),
+            pltpu.VMEM((width, 64), BF16),
             pltpu.VMEM((32, 8, width), BF16),
             pltpu.VMEM((8, 8, width), BF16),
             pltpu.VMEM((8, 8, width), BF16),
@@ -500,9 +504,9 @@
 
 
 def finish_kernel(w_ref, t_ref, w_out, t_out, sems):
-    half = [pl.ds(512 * i, 512) for i in range(2)]
-    copies = [pltpu.make_async_copy(w_ref.at[h], w_out.at[h], sems.at[i]) for i, h in enumerate(half)]
-    copies.append(pltpu.make_async_copy(t_ref, t_out, sems.at[2]))
+    eighth = [pl.ds(128 * i, 128) for i in range(8)]
+    copies = [pltpu.make_async_copy(w_ref.at[h], w_out.at[h], sems.at[i]) for i, h in enumerate(eighth)]
+    copies.append(pltpu.make_async_copy(t_ref, t_out, sems.at[8]))
     for cp in copies:
         cp.start()
     for cp in copies:
@@ -517,7 +521,7 @@
         out_shape=[jax.ShapeDtypeStruct(v.shape, v.dtype) for v in (wgrad, tgrad)],
         in_specs=[any_spec, any_spec],
         out_specs=[hbm, hbm],
-        scratch_shapes=[pltpu.SemaphoreType.DMA((3,))],
+        scratch_shapes=[pltpu.SemaphoreType.DMA((9,))],
         compiler_params=pltpu.CompilerParams(vmem_limit_bytes=1 << 20),
         name="finish",
     )(wgrad, tgrad)

time: 68.1 us -> 68.3 us (level)
  no operation moved by 1% of the time
where the time goes in v6:
time: 68.3 us; the launch traced here: 68.2 us
  Pallas kernels  66.4 us (97%)
  between operations  1.81 us (3%)
    pallas_call x1, Pallas kernels, step(): pl.pallas_call(step_kernel, out_shape=[jax.ShapeDtypeStruct((width, width...  65 us
    pallas_call x1, Pallas kernels, finish(): pl.pallas_call(finish_kernel, out_shape=[jax.ShapeDtypeStruct(v.shape, v....  1.39 us

profile of v6, /device:TPU:1, one launch (start us, length us, event | category | flops | bytes accessed | tf_op | source)
XLA Modules:
  0.0 68.2 jit_solution(3542302760889842712)
XLA Ops:
  0.6 65.0 %step.1 = (bf16[1024,1024]{1,0:T(8,128)(2,1)S(1)}, f32[8,1024]{1,0:T(8,128)S(1)}, f32[1,128]{1,0:T(1,128)S(1)}) custom-call(bf16[8,128,1024]{2,1,0:T(8,128)(2,1)} %feat_hbm.1, f32[1,1024]{1,0:T(1,128)} %bitcast.4, bf16[1024,1024]{1,0:T(8,128)(2,1)} %wq_hbm.1, bf16[1024,1024]{1,0:T(8,128)(2,1)} %wk_hbm.1, bf16[1024,1024]{1,0:T(8,128)(2,1)} %wv_hbm.1, ...), custom_call_target="tpu_custom_call" | custom-call | tf_op jit(solution)/shard_map/step/pallas_call | solution.py:456
  65.6 1.4 %finish.1 = (bf16[1024,1024]{1,0:T(8,128)(2,1)}, f32[8,1024]{1,0:T(8,128)}) custom-call(bf16[1024,1024]{1,0:T(8,128)(2,1)S(1)} %get-tuple-element.9.w_ref, f32[8,1024]{1,0:T(8,128)S(1)} %get-tuple-element.10.t_ref), custom_call_target="tpu_custom_call" | custom-call | tf_op jit(solution)/shard_map/finish/pallas_call | solution.py:519
